TPU v7x, 128 devices: a whole 4x4x4 slice. The times are simulated.
128 devices in a mesh: gz: 2 (over x_lo), gx: 2 (over core), gy: 32 (over z, y, x_hi).
Axes of the slice: x: 4 (x_hi: 2, x_lo: 2; x = x_hi * 2 + x_lo), y: 4, z: 4, core: 2. Of those that a mesh axis runs over, the one named last changes fastest.
Arguments:
- initial_field: float32 [128, 16, 4096], P('gz', 'gx', 'gy'), may hold values from -36 to 36
- plane_coupling: float32 [128, 16, 4096], P('gz', 'gx', 'gy'), may hold values from 0.06 to 0.24
- line_coupling: float32 [128, 16, 4096], P('gz', 'gx', 'gy'), may hold values from 1000 to 8000
- source: float32 [128, 16, 4096], P('gz', 'gx', 'gy'), may hold values from -4 to 4, as said below
- shift_table: float32 [8], replicated, may hold values from 0.5 to 1
- shift_index: int32 [4], replicated, may hold values from 0 to 7
Outputs:
- heated: float32 [128, 16, 4096], P('gz', 'gx', 'gy')
Inputs may be any that keep to these rules, and one draw needn't show every extreme that they name: `shift_index`: one table row for each half-step. A heat source.
All inputs are finite; a program needn't handle non-finite values.
Results may differ from a plain program's by a relative error of at most 0.0003.
Values sent between devices are 32-bit elements; how exact they have to be, the bound alone decides.
No kernel may reach another device: no remote copies, remote signals or barrier semaphores. Data moves between devices by JAX's collectives and lax.ppermute only.
A program may use at most 64 MiB of HBM per device.

v0:
```python
import functools

import jax
import jax.numpy as jnp
from jax import lax
from jax.experimental import pallas as pl
from jax.experimental.pallas import tpu as pltpu
from jax.sharding import PartitionSpec as P


HALF = 4
L = 64
ROWS = 8
COLS = 128
SWAP = [(0, 1), (1, 0)]
F32 = jnp.float32


def lanes():
    return lax.broadcasted_iota(jnp.int32, (ROWS, COLS), 1)


def subs():
    return lax.broadcasted_iota(jnp.int32, (ROWS, COLS), 0)


def roll(x, by):
    if isinstance(by, int):
        by = by % COLS
        return x if by == 0 else pltpu.roll(x, by, 1)
    return pltpu.roll(x, lax.rem(by + 2 * COLS, COLS), 1)


def layer(m):
    return m + lax.axis_index("gz") * (L - 1 - 2 * m)


class Rows:
    def __init__(self):
        gx = lax.axis_index("gx")
        sub = subs()
        low = jnp.where(gx == 0, 1.0, 0.0).astype(F32)
        high = 1.0 - low
        self.top = sub == 0
        self.bottom = sub == ROWS - 1
        self.low = jnp.full((ROWS, COLS), low, F32)
        self.high = jnp.full((ROWS, COLS), high, F32)

    def around(self, own, oth):
        a, b = pltpu.roll(own, 1, 0), pltpu.roll(oth, 1, 0)
        c, d = pltpu.roll(own, ROWS - 1, 0), pltpu.roll(oth, ROWS - 1, 0)
        own_sum = jnp.where(self.top, self.high * b, a) + jnp.where(self.bottom, self.low * d, c)
        oth_sum = jnp.where(self.top, self.low * a, b) + jnp.where(self.bottom, self.high * c, d)
        return (
            own_sum + (roll(own, 1) + roll(own, -1)),
            oth_sum + (roll(oth, 1) + roll(oth, -1)),
        )


def factor(inverse, inverse_shift, rest):
    x = inverse * inverse_shift + rest
    g = 1.0 / (1.0 + x)
    return g, x * g


def meet(d, rest, far_d, far_rest):
    far_g = 1.0 - far_rest
    return (far_d + far_g * d) / (rest + far_rest - rest * far_rest)


def load_kernel(u_in, p_in, l_in, s_in, table_in, index_in, u, p, l, s, ish, out, table, index, sem):
    into = (u, p, l, s, table, index)
    copies = [
        pltpu.make_async_copy(src, dst, sem.at[i])
        for i, (src, dst) in enumerate(zip((u_in, p_in, l_in, s_in, table_in, index_in), into))
    ]
    for copy in copies:
        copy.start()
    lane = lanes()
    copies[5].wait()
    copies[4].wait()
    for h in range(HALF):
        ish[h] = 1.0 / jnp.full((ROWS, COLS), table[index[h]], F32)
    for copy in copies[:4]:
        copy.wait()
    gz = lax.axis_index("gz")
    for q in range(L // 4):
        acc = None
        for i in range(4):
            k = layer(4 * q + i)
            for a, ref in enumerate((u, p, l, s)):
                at = 32 * i + 8 * a
                piece = roll(ref[k], at + 8 * (1 - gz))
                acc = piece if acc is None else jnp.where(lane >= at, piece, acc)
        out[q] = acc


def pack_side_kernel(u, p, l, s, z, out):
    lane = lanes()
    gz = lax.axis_index("gz")
    for q in range(L // 4):
        acc = None
        for half in range(2):
            for i in range(4):
                for a, ref in enumerate((u, p, l, s)):
                    at = 64 * half + 16 * i + 4 * a
                    if half == 0:
                        piece = roll(z[q], at - (32 * i + 8 * a) - 4 * gz)
                    else:
                        piece = roll(ref[layer(4 * q + i)], at + 4 * gz)
                    acc = piece if acc is None else jnp.where(lane >= at, piece, acc)
        out[q] = acc


def first_kernel(u, p, l, s, uo, po, lo, so, ish, g_out, c_out, d_out, pay):
    rows = Rows()
    shift = [ish[h] for h in range(HALF)]
    one = jnp.full((ROWS, COLS), 1.0, F32)
    zero = jnp.zeros((ROWS, COLS), F32)
    rest = [[one, one] for _ in range(HALF)]
    d = [zero, zero]
    for m in range(L):
        k = layer(m)
        fields = (u[k], uo[k])
        sums = rows.around(*fields)
        for x, (pr, lr, sr) in enumerate(((p, l, s), (po, lo, so))):
            inverse = 1.0 / lr[k]
            a1, a2 = inverse * pr[k], inverse * sr[k]
            c_out[0, x, m] = inverse
            c_out[1, x, m] = a1
            c_out[2, x, m] = a2
            f = fields[x] * (inverse * shift[0] - 4.0 * a1) + (a1 * sums[x] + a2)
            for h in range(HALF):
                g, rest[h][x] = factor(inverse, shift[h], rest[h][x])
                g_out[h, x, m] = g
                if h == 0:
                    d[x] = g * (d[x] + f)
                    d_out[x, m] = d[x]
    for x in range(2):
        pay[x] = d[x]
        for h in range(HALF):
            pay[2 + 2 * h + x] = rest[h][x]


def next_kernel(h, ish, g, c, d, rest, far_rest, far_d, d_out, pay, f_ref):
    rows = Rows()
    shift = ish[h]
    up = []
    for x in range(2):
        at = 2 + 2 * (h - 1) + x
        up.append(meet(d[x, L - 1], rest[at], far_d[x], far_rest[at]))
    for m in range(L - 1, -1, -1):
        up = [d[x, m] + g[h - 1, x, m] * up[x] for x in range(2)]
        sums = rows.around(*up)
        for x in range(2):
            inverse, a1, a2 = c[0, x, m], c[1, x, m], c[2, x, m]
            f_ref[x, m] = up[x] * (inverse * shift - 4.0 * a1) + (a1 * sums[x] + a2)
    now = [jnp.zeros((ROWS, COLS), F32)] * 2
    for m in range(L):
        for x in range(2):
            now[x] = g[h, x, m] * (now[x] + f_ref[x, m])
            d_out[x, m] = now[x]
    for x in range(2):
        pay[x] = now[x]


def last_kernel(g, d, rest, far_rest, far, edge, out):
    lane = lanes()
    gz = lax.axis_index("gz")
    at = 2 + 2 * (HALF - 1)
    up = meet(d[0, L - 1], rest[at], far[0], far_rest[at])
    zone = jnp.where(gz == 0, 0, COLS - 4)
    here = (lane >= zone) & (lane < zone + 4)
    other = COLS - 4 - zone
    there = (lane >= other) & (lane < other + 4)
    for m in range(L - 1, -1, -1):
        up = d[0, m] + g[HALF - 1, 0, m] * up
        v = jnp.where(here, roll(edge[m], -4 + 120 * gz), up)
        got = roll(far[1 + m // 32], other - 4 * (m % 32))
        out[layer(m)] = jnp.where(there, got, v)


def edge_local_kernel(u, p, l, s, uo, po, lo, so, z, zo, out):
    gz = lax.axis_index("gz")
    far = lanes() >= 64
    for m in range(L):
        k = layer(m)
        for x, refs in enumerate(((u, p, l, s, z), (uo, po, lo, so, zo))):
            for a in range(4):
                near = roll(refs[a][k], 4 + 8 * gz)
                beyond = roll(refs[4][m // 4], 68 - 32 * (m % 4) - 8 * a)
                out[a, x, m] = jnp.where(far, beyond, near)


def edge_first_kernel(v_ref, b, bo, ish, g_ref, c_ref, d_ref, rest_ref, w_ref):
    rows = Rows()
    gz = lax.axis_index("gz")
    gy = lax.axis_index("gy")
    within = lax.rem(lanes(), 64)
    inner = (within >= 4) & (within < 12)
    zone = 12 * gz
    halo = (within >= zone) & (within < zone + 4)
    open_side = jnp.where(gz == 0, gy > 0, gy < lax.axis_size("gy") - 1)
    keep = inner | (halo & open_side)
    shift = [ish[h] for h in range(HALF)]
    one = jnp.full((ROWS, COLS), 1.0, F32)
    zero = jnp.zeros((ROWS, COLS), F32)
    for m in range(L):
        for x, ref in enumerate((b, bo)):
            for a in range(4):
                v = jnp.where(halo, roll(ref[m // 4], zone - 16 * (m % 4) - 4 * a), v_ref[a, x, m])
                w_ref[a, x, m] = jnp.where(keep, v, one if a == 2 else zero)
    rest = [[one, one] for _ in range(HALF)]
    d = [zero, zero]
    for m in range(L):
        fields = [w_ref[0, x, m] for x in range(2)]
        sums = rows.around(*fields)
        for x in range(2):
            inverse = 1.0 / w_ref[2, x, m]
            a1, a2 = inverse * w_ref[1, x, m], inverse * w_ref[3, x, m]
            c_ref[0, x, m] = inverse
            c_ref[1, x, m] = a1
            c_ref[2, x, m] = a2
            f = fields[x] * (inverse * shift[0] - 4.0 * a1) + (a1 * sums[x] + a2)
            for h in range(HALF):
                g, rest[h][x] = factor(inverse, shift[h], rest[h][x])
                g_ref[h, x, m] = g
                if h == 0:
                    d[x] = g * (d[x] + f)
                    d_ref[x, m] = d[x]
    for x in range(2):
        for h in range(HALF):
            rest_ref[2 * h + x] = rest[h][x]


def edge_rest_kernel(g_ref, c_ref, d_in, rest_ref, ish, out, back, d_ref, f_ref):
    rows = Rows()
    lane = lanes()
    gz = lax.axis_index("gz")
    zero = jnp.zeros((ROWS, COLS), F32)
    d = [d_in[x, L - 1] for x in range(2)]
    for h in range(HALF):
        source = d_in if h == 0 else d_ref
        rest = [rest_ref[2 * h + x] for x in range(2)]
        up = [meet(d[x], rest[x], roll(d[x], 64), roll(rest[x], 64)) for x in range(2)]
        if h == HALF - 1:
            acc = zero
            for m in range(L - 1, -1, -1):
                up[0] = source[0, m] + g_ref[h, 0, m] * up[0]
                out[m] = up[0]
                at = 4 * (m % 32)
                acc = jnp.where(lane < at + 4, roll(up[0], at - 68 - 4 * gz), acc)
                if m % 32 == 0:
                    back[m // 32] = acc
            break
        for m in range(L - 1, -1, -1):
            up = [source[x, m] + g_ref[h, x, m] * up[x] for x in range(2)]
            sums = rows.around(*up)
            for x in range(2):
                inverse, a1, a2 = c_ref[0, x, m], c_ref[1, x, m], c_ref[2, x, m]
                f_ref[x, m] = up[x] * (inverse * ish[h + 1] - 4.0 * a1) + (a1 * sums[x] + a2)
        d = [zero, zero]
        for m in range(L):
            for x in range(2):
                d[x] = g_ref[h + 1, x, m] * (d[x] + f_ref[x, m])
                d_ref[x, m] = d[x]


def shape(*dims):
    return jax.ShapeDtypeStruct((*dims, ROWS, COLS), F32)


VMEM = pl.BlockSpec(memory_space=pltpu.VMEM)
HBM = pl.BlockSpec(memory_space=pltpu.HBM)


def call(body, outs, scratch=(), flops=1, specs=VMEM, limit=16 * 1024):
    def run(*args):
        return pl.pallas_call(
            body,
            out_shape=outs,
            in_specs=[specs] * len(args),
            out_specs=jax.tree.map(lambda _: VMEM, outs),
            scratch_shapes=[
                pltpu.VMEM(s.shape, s.dtype) if isinstance(s, jax.ShapeDtypeStruct) else s
                for s in scratch
            ],
            compiler_params=pltpu.CompilerParams(vmem_limit_bytes=limit * 1024),
            cost_estimate=pl.CostEstimate(flops=flops, bytes_accessed=0, transcendentals=0),
        )(*args)

    return run


def side_pairs(size):
    pairs = []
    for y in range(1, size):
        pairs += [(size + y - 1, y), (y, size + y - 1)]
    return pairs + [(i, i) for i in (0, 2 * size - 1)]


def on_device(initial_field, plane_coupling, line_coupling, source, shift_table, shift_index):
    size = lax.axis_size("gy")
    whole = shape(L)
    *own, ish, z_out = call(
        load_kernel,
        tuple(pltpu.VMEM(w.shape, F32) for w in (whole,) * 4 + (shape(HALF), shape(L // 4))),
        (
            pltpu.SMEM(shift_table.shape, F32),
            pltpu.SMEM(shift_index.shape, jnp.int32),
            pltpu.SemaphoreType.DMA((6,)),
        ),
        specs=HBM,
    )(
        *(
            pltpu.with_memory_space_constraint(a, pltpu.HBM)
            for a in (
                initial_field, plane_coupling, line_coupling, source, shift_table, shift_index
            )
        )
    )
    z_in = lax.ppermute(z_out, "gz", SWAP)
    oth = [lax.ppermute(a, "gx", SWAP) for a in own]

    g, c, d, pay = call(
        first_kernel, (shape(HALF, 2, L), shape(3, 2, L), shape(2, L), shape(10))
    )(*own, *oth, ish)
    rest = pay
    far = far_rest = lax.ppermute(pay, "gz", SWAP)

    z_oth = lax.ppermute(z_in, "gx", SWAP)
    out_b = call(pack_side_kernel, shape(L // 4))(*own, z_in)
    in_b = lax.ppermute(out_b, ("gz", "gy"), side_pairs(size))
    b_oth = lax.ppermute(in_b, "gx", SWAP)

    def step(h, d, far):
        return call(
            functools.partial(next_kernel, h), (shape(2, L), shape(2)), (shape(2, L),)
        )(ish, g, c, d, rest, far_rest, far)

    d, pay = step(1, d, far)
    far = lax.ppermute(pay, "gz", SWAP)
    local = call(edge_local_kernel, shape(4, 2, L))(*own, *oth, z_in, z_oth)
    d, pay = step(2, d, far)
    far = lax.ppermute(pay, "gz", SWAP)
    eg, ec, ed, er = call(
        edge_first_kernel,
        (shape(HALF, 2, L), shape(3, 2, L), shape(2, L), shape(2 * HALF)),
        (shape(4, 2, L),),
    )(local, in_b, b_oth, ish)
    edge, back = call(
        edge_rest_kernel, (whole, shape(2)), (shape(2, L), shape(2, L))
    )(eg, ec, ed, er, ish)
    d, pay = step(3, d, far)
    far = lax.ppermute(jnp.concatenate([pay[:1], back]), "gz", SWAP)
    return call(last_kernel, whole)(g, d, rest, far_rest, far, edge)


def solution(mesh):
    spec = P("gz", "gx", "gy")

    return jax.shard_map(
        on_device, mesh=mesh, in_specs=(spec,) * 4 + (P(), P()), out_specs=spec, check_vma=False
    )
```

profile of v0, /device:TPU:92, one launch (start us, length us, event | category | flops | bytes accessed | tf_op | source)
XLA Modules:
  0.0 38.6 jit_solution(18181915683849929828)
XLA Ops:
  0.0 1.6 %shard_map.64 = (f32[64,8,128]{2,1,0:T(8,128)S(1)}, f32[64,8,128]{2,1,0:T(8,128)S(1)}, f32[64,8,128]{2,1,0:T(8,128)S(1)}, f32[64,8,128]{2,1,0:T(8,128)S(1)}, f32...) custom-call(f32[64,8,128]{2,1,0:T(8,128)} %u_in.1, f32[64,8,128]{2,1,0:T(8,128)} %p_in.1, f32[64,8,128]{2,1,0:T(8,128)} %l_in.1, ...), custom_call_target="tpu_custom_call" | custom-call | flops 1 | tf_op jit(solution)/shard_map/pallas_call | solution.py:279
  1.6 0.1 collective-permute-start
  1.7 0.5 %collective-permute-start.1 = (f32[64,8,128]{2,1,0:T(8,128)S(1)}, f32[64,8,128]{2,1,0:T(8,128)S(1)}, u32[]{:S(2)}, u32[]{:S(2)}) collective-permute-start(f32[64,8,128]{2,1,0:T(8,128)S(1)} %get-tuple-element.28.p), channel_id=1, source_target_pairs={{0,32},{32,0},{1,33},{33,1},{2,34},{34,2},{3,35},{35,3},{4,36},{36... | collective-permute-start | bytes 786440 | tf_op jit(solution)/shard_map/ppermute | solution.py:323
  2.2 0.1 collective-permute-start.2
  2.3 0.4 %collective-permute-start.3 = (f32[64,8,128]{2,1,0:T(8,128)S(1)}, f32[64,8,128]{2,1,0:T(8,128)S(1)}, u32[]{:S(2)}, u32[]{:S(2)}) collective-permute-start(f32[64,8,128]{2,1,0:T(8,128)S(1)} %get-tuple-element.30.s), channel_id=1, source_target_pairs={{0,32},{32,0},{1,33},{33,1},{2,34},{34,2},{3,35},{35,3},{4,36},{36... | collective-permute-start | bytes 786440 | tf_op jit(solution)/shard_map/ppermute | solution.py:323
  2.7 1.2 %collective-permute-start.7 = (f32[16,8,128]{2,1,0:T(8,128)S(1)}, f32[16,8,128]{2,1,0:T(8,128)S(1)}, u32[]{:S(2)}, u32[]{:S(2)}) collective-permute-start(f32[16,8,128]{2,1,0:T(8,128)S(1)} %get-tuple-element.42), channel_id=1, source_target_pairs={{0,64},{64,0},{1,65},{65,1},{2,66},{66,2},{3,67},{67,3},{4,68},{68... | collective-permute-start | bytes 196616 | tf_op jit(solution)/shard_map/ppermute | solution.py:322
  3.9 3.1 %collective-permute-done.7.z = f32[16,8,128]{2,1,0:T(8,128)S(1)} collective-permute-done((f32[16,8,128]{2,1,0:T(8,128)S(1)}, f32[16,8,128]{2,1,0:T(8,128)S(1)}, u32[]{:S(2)}, u32[]{:S(2)}) %collective-permute-start.7) | collective-permute-done | bytes 65568 | tf_op jit(solution)/shard_map/ppermute | solution.py:322
  7.0 0.6 %shard_map.70 = f32[16,8,128]{2,1,0:T(8,128)S(1)} custom-call(f32[64,8,128]{2,1,0:T(8,128)S(1)} %get-tuple-element.27.u, f32[64,8,128]{2,1,0:T(8,128)S(1)} %get-tuple-element.28.p, f32[64,8,128]{2,1,0:T(8,128)S(1)} %get-tuple-element.29.l, f32[64,8,128]{2,1,0:T(8,128)S(1)} %get-tuple-element.30.s, f32[16,8,128]{2,1,0:T(8,128)S(1)} %collective-permute-done.7.z), custom_call_target="tpu_custom_call" | custom-call | flops 1 | tf_op jit(solution)/shard_map/pallas_call | solution.py:279
  7.6 2.4 %collective-permute-start.9 = (f32[16,8,128]{2,1,0:T(8,128)S(1)}, f32[16,8,128]{2,1,0:T(8,128)S(1)}, u32[]{:S(2)}, u32[]{:S(2)}) collective-permute-start(f32[16,8,128]{2,1,0:T(8,128)S(1)} %shard_map.70), channel_id=1, source_target_pairs={{64,1},{1,64},{65,2},{2,65},{66,3},{3,66},{67,4},{4,67},{68,5},{5,... | collective-permute-start | bytes 196616 | tf_op jit(solution)/shard_map/ppermute | solution.py:333
  10.0 3.7 %collective-permute-done.9.b = f32[16,8,128]{2,1,0:T(8,128)S(1)} collective-permute-done((f32[16,8,128]{2,1,0:T(8,128)S(1)}, f32[16,8,128]{2,1,0:T(8,128)S(1)}, u32[]{:S(2)}, u32[]{:S(2)}) %collective-permute-start.9) | collective-permute-done | bytes 65568 | tf_op jit(solution)/shard_map/ppermute | solution.py:333
  13.7 0.0 collective-permute-start.8
  13.7 0.0 collective-permute-done.uo
  13.8 0.5 %collective-permute-start.10 = (f32[16,8,128]{2,1,0:T(8,128)S(1)}, f32[16,8,128]{2,1,0:T(8,128)S(1)}, u32[]{:S(2)}, u32[]{:S(2)}) collective-permute-start(f32[16,8,128]{2,1,0:T(8,128)S(1)} %collective-permute-done.9.b), channel_id=1, source_target_pairs={{0,32},{32,0},{1,33},{33,1},{2,34},{34,2},{3,35},{35,3},{4,36},{36... | collective-permute-start | bytes 196616 | tf_op jit(solution)/shard_map/ppermute | solution.py:334
  14.3 0.0 collective-permute-done.1.po
  14.3 0.0 collective-permute-done.2.lo
  14.3 0.0 collective-permute-done.3.so
  14.3 0.8 %shard_map.65 = (f32[4,2,64,8,128]{4,3,2,1,0:T(8,128)S(1)}, f32[3,2,64,8,128]{4,3,2,1,0:T(8,128)S(1)}, f32[2,64,8,128]{3,2,1,0:T(8,128)S(1)}, f32[10,8,128]{2,1,0:T(8,128)S(1)}) custom-call(f32[64,8,128]{2,1,0:T(8,128)S(1)} %get-tuple-element.27.u, f32[64,8,128]{2,1,0:T(8,128)S(1)} %get-tuple-element.28.p, f32[64,8,128]{2,1,0:T(8,128)S(1)} %get-tuple-element.29.l, ...), custom_call_target="tpu_custom_call" | custom-call | flops 1 | tf_op jit(solution)/shard_map/pallas_call | solution.py:279
  15.1 5.5 %collective-permute-start.4 = (f32[10,8,128]{2,1,0:T(8,128)S(1)}, f32[10,8,128]{2,1,0:T(8,128)S(1)}, u32[]{:S(2)}, u32[]{:S(2)}) collective-permute-start(f32[10,8,128]{2,1,0:T(8,128)S(1)} %get-tuple-element.35.rest), channel_id=1, source_target_pairs={{0,64},{64,0},{1,65},{65,1},{2,66},{66,2},{3,67},{67,3},{4,68},{68... | collective-permute-start | bytes 122888 | tf_op jit(solution)/shard_map/ppermute | solution.py:329
  20.6 2.0 %collective-permute-done.4.far_rest.far_d = f32[10,8,128]{2,1,0:T(8,128)S(1)} collective-permute-done((f32[10,8,128]{2,1,0:T(8,128)S(1)}, f32[10,8,128]{2,1,0:T(8,128)S(1)}, u32[]{:S(2)}, u32[]{:S(2)}) %collective-permute-start.4) | collective-permute-done | bytes 40992 | tf_op jit(solution)/shard_map/ppermute | solution.py:329
  22.6 0.4 %shard_map.66 = (f32[2,64,8,128]{3,2,1,0:T(8,128)S(1)}, f32[2,8,128]{2,1,0:T(8,128)S(1)}) custom-call(f32[4,8,128]{2,1,0:T(8,128)S(1)} %get-tuple-element.31.ish, f32[4,2,64,8,128]{4,3,2,1,0:T(8,128)S(1)} %get-tuple-element.32.g, f32[3,2,64,8,128]{4,3,2,1,0:T(8,128)S(1)} %get-tuple-element.33.c, f32[2,64,8,128]{3,2,1,0:T(8,128)S(1)} %get-tuple-element.34.d, ...), custom_call_target="tpu_custom_call" | custom-call | flops 1 | tf_op jit(solution)/shard_map/pallas_call | solution.py:279
  23.1 2.1 %collective-permute-start.5 = (f32[2,8,128]{2,1,0:T(8,128)S(1)}, f32[2,8,128]{2,1,0:T(8,128)S(1)}, u32[]{:S(2)}, u32[]{:S(2)}) collective-permute-start(f32[2,8,128]{2,1,0:T(8,128)S(1)} %get-tuple-element.37), channel_id=1, source_target_pairs={{0,64},{64,0},{1,65},{65,1},{2,66},{66,2},{3,67},{67,3},{4,68},{68... | collective-permute-start | bytes 24584 | tf_op jit(solution)/shard_map/ppermute | solution.py:342
  25.2 1.6 %collective-permute-done.5.far_d = f32[2,8,128]{2,1,0:T(8,128)S(1)} collective-permute-done((f32[2,8,128]{2,1,0:T(8,128)S(1)}, f32[2,8,128]{2,1,0:T(8,128)S(1)}, u32[]{:S(2)}, u32[]{:S(2)}) %collective-permute-start.5) | collective-permute-done | bytes 8224 | tf_op jit(solution)/shard_map/ppermute | solution.py:342
  26.8 0.4 %shard_map.67 = (f32[2,64,8,128]{3,2,1,0:T(8,128)S(1)}, f32[2,8,128]{2,1,0:T(8,128)S(1)}) custom-call(f32[4,8,128]{2,1,0:T(8,128)S(1)} %get-tuple-element.31.ish, f32[4,2,64,8,128]{4,3,2,1,0:T(8,128)S(1)} %get-tuple-element.32.g, f32[3,2,64,8,128]{4,3,2,1,0:T(8,128)S(1)} %get-tuple-element.33.c, f32[2,64,8,128]{3,2,1,0:T(8,128)S(1)} %get-tuple-element.36.d, ...), custom_call_target="tpu_custom_call" | custom-call | flops 1 | tf_op jit(solution)/shard_map/pallas_call | solution.py:279
  27.2 2.1 %collective-permute-start.6 = (f32[2,8,128]{2,1,0:T(8,128)S(1)}, f32[2,8,128]{2,1,0:T(8,128)S(1)}, u32[]{:S(2)}, u32[]{:S(2)}) collective-permute-start(f32[2,8,128]{2,1,0:T(8,128)S(1)} %get-tuple-element.39), channel_id=1, source_target_pairs={{0,64},{64,0},{1,65},{65,1},{2,66},{66,2},{3,67},{67,3},{4,68},{68... | collective-permute-start | bytes 24584 | tf_op jit(solution)/shard_map/ppermute | solution.py:345
  29.3 0.0 collective-permute-done.8.zo
  29.3 1.2 %shard_map.69.v_ref = f32[4,2,64,8,128]{4,3,2,1,0:T(8,128)S(1)} custom-call(f32[64,8,128]{2,1,0:T(8,128)S(1)} %get-tuple-element.27.u, f32[64,8,128]{2,1,0:T(8,128)S(1)} %get-tuple-element.28.p, f32[64,8,128]{2,1,0:T(8,128)S(1)} %get-tuple-element.29.l, f32[64,8,128]{2,1,0:T(8,128)S(1)} %get-tuple-element.30.s, f32[64,8,128]{2,1,0:T(8,128)S(1)} %collective-permute-done.uo, ...), custom_call_target="tpu_custom_call" | custom-call | flops 1 | tf_op jit(solution)/shard_map/pallas_call | solution.py:279
  30.5 0.0 collective-permute-done.10.bo
  30.5 1.2 %shard_map.71 = (f32[4,2,64,8,128]{4,3,2,1,0:T(8,128)S(1)}, f32[3,2,64,8,128]{4,3,2,1,0:T(8,128)S(1)}, f32[2,64,8,128]{3,2,1,0:T(8,128)S(1)}, f32[8,8,128]{2,1,0:T(8,128)S(1)}) custom-call(f32[4,2,64,8,128]{4,3,2,1,0:T(8,128)S(1)} %shard_map.69.v_ref, f32[16,8,128]{2,1,0:T(8,128)S(1)} %collective-permute-done.9.b, ...), custom_call_target="tpu_custom_call" | custom-call | flops 1 | tf_op jit(solution)/shard_map/pallas_call | solution.py:279
  31.7 1.7 %shard_map.72 = (f32[64,8,128]{2,1,0:T(8,128)S(1)}, f32[2,8,128]{2,1,0:T(8,128)S(1)}) custom-call(f32[4,2,64,8,128]{4,3,2,1,0:T(8,128)S(1)} %get-tuple-element.43.g_ref, f32[3,2,64,8,128]{4,3,2,1,0:T(8,128)S(1)} %get-tuple-element.44.c_ref, f32[2,64,8,128]{3,2,1,0:T(8,128)S(1)} %get-tuple-element.45.d_in, f32[8,8,128]{2,1,0:T(8,128)S(1)} %get-tuple-element.46.rest_ref, ...), custom_call_target="tpu_custom_call" | custom-call | flops 1 | tf_op jit(solution)/shard_map/pallas_call | solution.py:279
  33.4 0.0 collective-permute-done.6.far_d
  33.4 0.4 %shard_map.68 = (f32[2,64,8,128]{3,2,1,0:T(8,128)S(1)}, f32[2,8,128]{2,1,0:T(8,128)S(1)}) custom-call(f32[4,8,128]{2,1,0:T(8,128)S(1)} %get-tuple-element.31.ish, f32[4,2,64,8,128]{4,3,2,1,0:T(8,128)S(1)} %get-tuple-element.32.g, f32[3,2,64,8,128]{4,3,2,1,0:T(8,128)S(1)} %get-tuple-element.33.c, f32[2,64,8,128]{3,2,1,0:T(8,128)S(1)} %get-tuple-element.38.d, ...), custom_call_target="tpu_custom_call" | custom-call | flops 1 | tf_op jit(solution)/shard_map/pallas_call | solution.py:279
  33.9 0.1 collective-permute-start.11
  34.0 3.7 %collective-permute-done.11.far = f32[3,8,128]{2,1,0:T(8,128)S(1)} collective-permute-done((f32[3,8,128]{2,1,0:T(8,128)S(1)}, f32[3,8,128]{2,1,0:T(8,128)S(1)}, u32[]{:S(2)}, u32[]{:S(2)}) %collective-permute-start.11) | collective-permute-done | bytes 12320 | tf_op jit(solution)/shard_map/ppermute | solution.py:355
  37.6 0.9 %shard_map.73 = f32[64,8,128]{2,1,0:T(8,128)} custom-call(f32[4,2,64,8,128]{4,3,2,1,0:T(8,128)S(1)} %get-tuple-element.32.g, f32[2,64,8,128]{3,2,1,0:T(8,128)S(1)} %get-tuple-element.40.d, f32[10,8,128]{2,1,0:T(8,128)S(1)} %get-tuple-element.35.rest, f32[10,8,128]{2,1,0:T(8,128)S(1)} %collective-permute-done.4.far_rest.far_d, ...), custom_call_target="tpu_custom_call" | custom-call | flops 1 | tf_op jit(solution)/shard_map/pallas_call | solution.py:279
  (2 shorter events, 0.0 us)
Async XLA Ops:
  1.6 12.2 %collective-permute-start = (f32[64,8,128]{2,1,0:T(8,128)S(1)}, f32[64,8,128]{2,1,0:T(8,128)S(1)}, u32[]{:S(2)}, u32[]{:S(2)}) collective-permute-start(f32[64,8,128]{2,1,0:T(8,128)S(1)} %get-tuple-element.27.u), channel_id=1, source_target_pairs={{0,32},{32,0},{1,33},{33,1},{2,34},{34,2},{3,35},{35,3},{4,36},{36... | collective-permute-start | bytes 786440 | tf_op jit(solution)/shard_map/ppermute | solution.py:323
  1.7 12.6 %collective-permute-start.1 = (f32[64,8,128]{2,1,0:T(8,128)S(1)}, f32[64,8,128]{2,1,0:T(8,128)S(1)}, u32[]{:S(2)}, u32[]{:S(2)}) collective-permute-start(f32[64,8,128]{2,1,0:T(8,128)S(1)} %get-tuple-element.28.p), channel_id=1, source_target_pairs={{0,32},{32,0},{1,33},{33,1},{2,34},{34,2},{3,35},{35,3},{4,36},{36... | collective-permute-start | bytes 786440 | tf_op jit(solution)/shard_map/ppermute | solution.py:323
  2.2 12.1 %collective-permute-start.2 = (f32[64,8,128]{2,1,0:T(8,128)S(1)}, f32[64,8,128]{2,1,0:T(8,128)S(1)}, u32[]{:S(2)}, u32[]{:S(2)}) collective-permute-start(f32[64,8,128]{2,1,0:T(8,128)S(1)} %get-tuple-element.29.l), channel_id=1, source_target_pairs={{0,32},{32,0},{1,33},{33,1},{2,34},{34,2},{3,35},{35,3},{4,36},{36... | collective-permute-start | bytes 786440 | tf_op jit(solution)/shard_map/ppermute | solution.py:323
  2.3 12.0 %collective-permute-start.3 = (f32[64,8,128]{2,1,0:T(8,128)S(1)}, f32[64,8,128]{2,1,0:T(8,128)S(1)}, u32[]{:S(2)}, u32[]{:S(2)}) collective-permute-start(f32[64,8,128]{2,1,0:T(8,128)S(1)} %get-tuple-element.30.s), channel_id=1, source_target_pairs={{0,32},{32,0},{1,33},{33,1},{2,34},{34,2},{3,35},{35,3},{4,36},{36... | collective-permute-start | bytes 786440 | tf_op jit(solution)/shard_map/ppermute | solution.py:323
  2.7 4.3 %collective-permute-start.7 = (f32[16,8,128]{2,1,0:T(8,128)S(1)}, f32[16,8,128]{2,1,0:T(8,128)S(1)}, u32[]{:S(2)}, u32[]{:S(2)}) collective-permute-start(f32[16,8,128]{2,1,0:T(8,128)S(1)} %get-tuple-element.42), channel_id=1, source_target_pairs={{0,64},{64,0},{1,65},{65,1},{2,66},{66,2},{3,67},{67,3},{4,68},{68... | collective-permute-start | bytes 196616 | tf_op jit(solution)/shard_map/ppermute | solution.py:322
  7.6 6.2 %collective-permute-start.9 = (f32[16,8,128]{2,1,0:T(8,128)S(1)}, f32[16,8,128]{2,1,0:T(8,128)S(1)}, u32[]{:S(2)}, u32[]{:S(2)}) collective-permute-start(f32[16,8,128]{2,1,0:T(8,128)S(1)} %shard_map.70), channel_id=1, source_target_pairs={{64,1},{1,64},{65,2},{2,65},{66,3},{3,66},{67,4},{4,67},{68,5},{5,... | collective-permute-start | bytes 196616 | tf_op jit(solution)/shard_map/ppermute | solution.py:333
  13.7 15.6 %collective-permute-start.8 = (f32[16,8,128]{2,1,0:T(8,128)S(1)}, f32[16,8,128]{2,1,0:T(8,128)S(1)}, u32[]{:S(2)}, u32[]{:S(2)}) collective-permute-start(f32[16,8,128]{2,1,0:T(8,128)S(1)} %collective-permute-done.7.z), channel_id=1, source_target_pairs={{0,32},{32,0},{1,33},{33,1},{2,34},{34,2},{3,35},{35,3},{4,36},{36... | collective-permute-start | bytes 196616 | tf_op jit(solution)/shard_map/ppermute | solution.py:331
  13.8 16.7 %collective-permute-start.10 = (f32[16,8,128]{2,1,0:T(8,128)S(1)}, f32[16,8,128]{2,1,0:T(8,128)S(1)}, u32[]{:S(2)}, u32[]{:S(2)}) collective-permute-start(f32[16,8,128]{2,1,0:T(8,128)S(1)} %collective-permute-done.9.b), channel_id=1, source_target_pairs={{0,32},{32,0},{1,33},{33,1},{2,34},{34,2},{3,35},{35,3},{4,36},{36... | collective-permute-start | bytes 196616 | tf_op jit(solution)/shard_map/ppermute | solution.py:334
  15.1 7.5 %collective-permute-start.4 = (f32[10,8,128]{2,1,0:T(8,128)S(1)}, f32[10,8,128]{2,1,0:T(8,128)S(1)}, u32[]{:S(2)}, u32[]{:S(2)}) collective-permute-start(f32[10,8,128]{2,1,0:T(8,128)S(1)} %get-tuple-element.35.rest), channel_id=1, source_target_pairs={{0,64},{64,0},{1,65},{65,1},{2,66},{66,2},{3,67},{67,3},{4,68},{68... | collective-permute-start | bytes 122888 | tf_op jit(solution)/shard_map/ppermute | solution.py:329
  23.1 3.7 %collective-permute-start.5 = (f32[2,8,128]{2,1,0:T(8,128)S(1)}, f32[2,8,128]{2,1,0:T(8,128)S(1)}, u32[]{:S(2)}, u32[]{:S(2)}) collective-permute-start(f32[2,8,128]{2,1,0:T(8,128)S(1)} %get-tuple-element.37), channel_id=1, source_target_pairs={{0,64},{64,0},{1,65},{65,1},{2,66},{66,2},{3,67},{67,3},{4,68},{68... | collective-permute-start | bytes 24584 | tf_op jit(solution)/shard_map/ppermute | solution.py:342
  27.2 6.2 %collective-permute-start.6 = (f32[2,8,128]{2,1,0:T(8,128)S(1)}, f32[2,8,128]{2,1,0:T(8,128)S(1)}, u32[]{:S(2)}, u32[]{:S(2)}) collective-permute-start(f32[2,8,128]{2,1,0:T(8,128)S(1)} %get-tuple-element.39), channel_id=1, source_target_pairs={{0,64},{64,0},{1,65},{65,1},{2,66},{66,2},{3,67},{67,3},{4,68},{68... | collective-permute-start | bytes 24584 | tf_op jit(solution)/shard_map/ppermute | solution.py:345
  33.9 3.8 %collective-permute-start.11 = (f32[3,8,128]{2,1,0:T(8,128)S(1)}, f32[3,8,128]{2,1,0:T(8,128)S(1)}, u32[]{:S(2)}, u32[]{:S(2)}) collective-permute-start(f32[3,8,128]{2,1,0:T(8,128)S(1)} %pad_maximum_fusion), channel_id=1, source_target_pairs={{0,64},{64,0},{1,65},{65,1},{2,66},{66,2},{3,67},{67,3},{4,68},{68... | collective-permute-start | bytes 36872 | tf_op jit(solution)/shard_map/ppermute | solution.py:355
where the time goes:
time: 38.7 us; the launch traced here: 38.6 us
  starting transfers between devices  15.1 us (39%)
  waiting for transfers between devices  14.1 us (36%)
  Pallas kernels  9.31 us (24%)
    pallas_call x10, Pallas kernels, run(): pl.pallas_call(body, out_shape=outs, in_specs=[specs] * len(args), out_sp...  9.31 us
    ppermute x1, starting transfers between devices, on_device(): far = far_rest = lax.ppermute(pay, 'gz', SWAP)  5.51 us
    ppermute x2, starting transfers between devices, on_device(): far = lax.ppermute(pay, 'gz', SWAP)  4.2 us
    ppermute x1, waiting for transfers between devices, on_device(): in_b = lax.ppermute(out_b, ('gz', 'gy'), side_pairs(size))  3.71 us
    ppermute x1, waiting for transfers between devices, on_device(): far = lax.ppermute(jnp.concatenate([pay[:1], back]), 'gz', SWAP)  3.67 us
    ppermute x1, waiting for transfers between devices, on_device(): z_in = lax.ppermute(z_out, 'gz', SWAP)  3.07 us
    ppermute x1, starting transfers between devices, on_device(): in_b = lax.ppermute(out_b, ('gz', 'gy'), side_pairs(size))  2.44 us
    ppermute x1, waiting for transfers between devices, on_device(): far = far_rest = lax.ppermute(pay, 'gz', SWAP)  1.98 us
  transfers between devices with their start and end apart: 12, of which 5 were waited for; matrix products, arithmetic and copies ran while one was open for 0% of the time, Pallas kernels for 17%

commit v1 on v0

v1 whole, which is shorter than its diff:
```python
import jax
import jax.numpy as jnp
from jax import lax
from jax.experimental import pallas as pl
from jax.experimental.pallas import tpu as pltpu
from jax.sharding import PartitionSpec as P


HALF = 4
CHUNK = 16
L = 64
ROWS = 8
COLS = 128
SWAP = [(0, 1), (1, 0)]
CROSS = [(i, 3 - i) for i in range(4)]
ZX = ("gz", "gx")
F32 = jnp.float32


def lanes():
    return lax.broadcasted_iota(jnp.int32, (ROWS, COLS), 1)


def subs():
    return lax.broadcasted_iota(jnp.int32, (ROWS, COLS), 0)


def roll(x, by):
    if isinstance(by, int):
        by = by % COLS
        return x if by == 0 else pltpu.roll(x, by, 1)
    return pltpu.roll(x, lax.rem(by + 2 * COLS, COLS), 1)


def layer(m):
    return m + lax.axis_index("gz") * (L - 1 - 2 * m)


def zone_side():
    return 1 - lax.axis_index("gz")


class Rows:
    def __init__(self):
        gx = lax.axis_index("gx")
        sub = subs()
        low = jnp.where(gx == 0, 1.0, 0.0).astype(F32)
        high = 1.0 - low
        self.top = sub == 0
        self.bottom = sub == ROWS - 1
        self.low = jnp.full((ROWS, COLS), low, F32)
        self.high = jnp.full((ROWS, COLS), high, F32)

    def beside(self, own, oth):
        a, b = pltpu.roll(own, 1, 0), pltpu.roll(oth, 1, 0)
        c, d = pltpu.roll(own, ROWS - 1, 0), pltpu.roll(oth, ROWS - 1, 0)
        return (
            (
                jnp.where(self.top, self.high * b, a),
                jnp.where(self.bottom, self.low * d, c),
                roll(own, 1),
                roll(own, -1),
            ),
            (
                jnp.where(self.top, self.low * a, b),
                jnp.where(self.bottom, self.high * c, d),
                roll(oth, 1),
                roll(oth, -1),
            ),
        )

    def around(self, own, oth):
        return tuple((n[0] + n[1]) + (n[2] + n[3]) for n in self.beside(own, oth))


def factor(inverse, inverse_shift, before):
    p, e = before
    e = e + (inverse * inverse_shift) * p
    after = p + e
    return p * (1.0 / after), (after, e)


def meet(d, rest, far_d, far_rest):
    far_g = 1.0 - far_rest
    return (far_d + far_g * d) / (rest + far_rest - rest * far_rest)


def forcing(own, around, inverse, a1, a2, shift):
    return own * (inverse * shift - 4.0 * a1) + (a1 * around + a2)


def explicit(rows, up, c, m, shift, f_ref, which=(0, 1)):
    sums = rows.around(*up)
    for x in which:
        f_ref[x, m] = forcing(up[x], sums[x], c[0, x, m], c[1, x, m], c[2, x, m], shift)


def reach(h, rows, shift, g, c, d, which):
    one = jnp.full((ROWS, COLS), 1.0, F32)
    zero = jnp.zeros((ROWS, COLS), F32)
    up, to, on = [zero] * 2, [one] * 2, [one] * 2
    total = [[zero] * 6 for _ in range(2)]
    for m in range(L - 1, -1, -1):
        for x in range(2):
            up[x] = d[x, m] + g[h, x, m] * up[x]
            to[x] = to[x] * g[h, x, m]
        around = rows.around(*up)
        beside = rows.beside(*to)
        for x in which:
            on[x] = on[x] * g[h + 1, x, m]
            inverse, a1, a2 = c[0, x, m], c[1, x, m], c[2, x, m]
            middle = inverse * shift - 4.0 * a1
            f = up[x] * middle + (a1 * around[x] + a2)
            weight = on[x] * a1
            add = [on[x] * f, on[x] * middle * to[x]] + [weight * n for n in beside[x]]
            total[x] = [t + v for t, v in zip(total[x], add)]
    return total


def reached(rows, total, last):
    beside = rows.beside(*last)
    found = []
    for x in range(2):
        t = total[x]
        value = None
        if t is not None:
            value = t(0) + t(1) * last[x]
            for i in range(4):
                value = value + t(2 + i) * beside[x][i]
        found.append(value)
    return found


def load_kernel(u_in, p_in, l_in, s_in, table_in, index_in, u, p, l, s, ish, out, table, index, sem):
    into = (u, p, l, s, table, index)
    copies = [
        pltpu.make_async_copy(src, dst, sem.at[i])
        for i, (src, dst) in enumerate(zip((u_in, p_in, l_in, s_in, table_in, index_in), into))
    ]
    for copy in copies:
        copy.start()
    lane = lanes()
    copies[5].wait()
    copies[4].wait()
    for h in range(HALF):
        ish[h] = 1.0 / jnp.full((ROWS, COLS), table[index[h]], F32)
    for copy in copies[:4]:
        copy.wait()
    side = zone_side()
    for q in range(L // 4):
        acc = None
        for i in range(4):
            k = layer(4 * q + i)
            for a, ref in enumerate((u, p, l, s)):
                at = 32 * i + 8 * a
                piece = roll(ref[k], at + 8 * (1 - side))
                acc = piece if acc is None else jnp.where(lane >= at, piece, acc)
        out[q] = acc


def pack_side_kernel(u, p, l, s, z, out):
    lane = lanes()
    side = zone_side()
    for q in range(L // 4):
        acc = None
        for half in range(2):
            for i in range(4):
                for a, ref in enumerate((u, p, l, s)):
                    at = 64 * half + 16 * i + 4 * a
                    if half == 0:
                        piece = roll(z[q], at - (32 * i + 8 * a) - 4 * side)
                    else:
                        piece = roll(ref[layer(4 * q + i)], at + 4 * side)
                    acc = piece if acc is None else jnp.where(lane >= at, piece, acc)
        out[q] = acc


def first_kernel(u, p, l, s, uo, po, lo, so, ish, g_out, c_out, d_out, rest_out, pay):
    rows = Rows()
    shift = [ish[h] for h in range(HALF)]
    one = jnp.full((ROWS, COLS), 1.0, F32)
    zero = jnp.zeros((ROWS, COLS), F32)
    rest = [[(one, one)] * 2 for _ in range(HALF)]
    d = [zero, zero]
    for m in range(L):
        k = layer(m)
        fields = (u[k], uo[k])
        sums = rows.around(*fields)
        for x, (pr, lr, sr) in enumerate(((p, l, s), (po, lo, so))):
            inverse = 1.0 / lr[k]
            a1, a2 = inverse * pr[k], inverse * sr[k]
            c_out[0, x, m] = inverse
            c_out[1, x, m] = a1
            c_out[2, x, m] = a2
            f = forcing(fields[x], sums[x], inverse, a1, a2, shift[0])
            for h in range(HALF):
                g, rest[h][x] = factor(inverse, shift[h], rest[h][x])
                g_out[h, x, m] = g
                if h == 0:
                    d[x] = g * (d[x] + f)
                    d_out[x, m] = d[x]
    total = reach(0, rows, shift[1], g_out, c_out, d_out, (0, 1))
    for x in range(2):
        pay[x] = d[x]
        for h in range(HALF):
            p, e = rest[h][x]
            rest_out[2 * h + x] = e / p
            pay[2 + 2 * h + x] = e / p
        for i in range(6):
            pay[10 + 6 * x + i] = total[x][i]


def middle_kernel(ish, g, c, d, rest, far, d_out, pay, f_ref, d_ref):
    rows = Rows()
    zero = jnp.zeros((ROWS, COLS), F32)

    def far_rest(h, x):
        return far[2 + 2 * h + 1 - x]

    up = [meet(d[x, L - 1], rest[x], far[1 - x], far_rest(0, x)) for x in range(2)]
    for m in range(L - 1, -1, -1):
        up = [d[x, m] + g[0, x, m] * up[x] for x in range(2)]
        if m == L - 1:
            last = up
        explicit(rows, up, c, m, ish[1], f_ref)
    now = [zero, zero]
    for m in range(L):
        for x in range(2):
            now[x] = g[1, x, m] * (now[x] + f_ref[x, m])
            d_ref[x, m] = now[x]
    far_d = reached(rows, [lambda i, x=x: far[10 + 6 * (1 - x) + i] for x in range(2)], last)
    up = [meet(now[x], rest[2 + x], far_d[x], far_rest(1, x)) for x in range(2)]
    for m in range(L - 1, -1, -1):
        up = [d_ref[x, m] + g[1, x, m] * up[x] for x in range(2)]
        explicit(rows, up, c, m, ish[2], f_ref)
    now = [zero, zero]
    for m in range(L):
        for x in range(2):
            now[x] = g[2, x, m] * (now[x] + f_ref[x, m])
            d_out[x, m] = now[x]
    total = reach(2, rows, ish[3], g, c, d_out, (1,))
    for x in range(2):
        pay[x] = now[x]
    for i in range(6):
        pay[2 + i] = total[1][i]


def last_kernel(ish, g, c, d, rest, far_rest, far, edge, out, field, f_ref, d_ref, sem):
    lane = lanes()
    rows = Rows()
    gz = lax.axis_index("gz")
    side = zone_side()
    up = [meet(d[x, L - 1], rest[4 + x], far[1 - x], far_rest[6 + 1 - x]) for x in range(2)]
    for m in range(L - 1, -1, -1):
        up = [d[x, m] + g[2, x, m] * up[x] for x in range(2)]
        if m == L - 1:
            last = up
        explicit(rows, up, c, m, ish[3], f_ref, (0,))
    now = jnp.zeros((ROWS, COLS), F32)
    for m in range(L):
        now = g[3, 0, m] * (now + f_ref[0, m])
        d_ref[m] = now
    far_d = reached(rows, [lambda i: far[2 + i], None], last)[0]
    up = meet(now, rest[6], far_d, far_rest[8 + 1])
    zone = jnp.where(side == 0, 0, COLS - 4)
    here = (lane >= zone) & (lane < zone + 4)
    other = COLS - 4 - zone
    there = (lane >= other) & (lane < other + 4)
    copies = []
    for m in range(L - 1, -1, -1):
        up = d_ref[m] + g[HALF - 1, 0, m] * up
        v = jnp.where(here, roll(edge[m], -4 + 120 * side), up)
        got = roll(far[8 + m // 32], other - 4 * (m % 32))
        field[layer(m)] = jnp.where(there, got, v)
        if m % CHUNK == 0:
            start = jnp.where(gz == 0, m, L - CHUNK - m)
            part = pl.ds(start, CHUNK)
            copies.append(pltpu.make_async_copy(field.at[part], out.at[part], sem.at[m // CHUNK]))
            copies[-1].start()
    for copy in copies:
        copy.wait()


def edge_local_kernel(u, p, l, s, uo, po, lo, so, z, zo, out):
    side = zone_side()
    far = lanes() >= 64
    for m in range(L):
        k = layer(m)
        for x, refs in enumerate(((u, p, l, s, z), (uo, po, lo, so, zo))):
            for a in range(4):
                near = roll(refs[a][k], 4 + 8 * side)
                beyond = roll(refs[4][m // 4], 68 - 32 * (m % 4) - 8 * a)
                out[a, x, m] = jnp.where(far, beyond, near)


def edge_first_kernel(v_ref, b, bo, ish, g_ref, c_ref, d_ref, rest_ref, w_ref):
    rows = Rows()
    side = zone_side()
    gy = lax.axis_index("gy")
    within = lax.rem(lanes(), 64)
    inner = (within >= 4) & (within < 12)
    zone = 12 * side
    halo = (within >= zone) & (within < zone + 4)
    open_side = jnp.where(side == 0, gy > 0, gy < lax.axis_size("gy") - 1)
    keep = inner | (halo & open_side)
    shift = [ish[h] for h in range(HALF)]
    one = jnp.full((ROWS, COLS), 1.0, F32)
    zero = jnp.zeros((ROWS, COLS), F32)
    for m in range(L):
        for x, ref in enumerate((b, bo)):
            for a in range(4):
                v = jnp.where(halo, roll(ref[m // 4], zone - 16 * (m % 4) - 4 * a), v_ref[a, x, m])
                w_ref[a, x, m] = jnp.where(keep, v, 1000.0 * one if a == 2 else zero)
    rest = [[(one, one)] * 2 for _ in range(HALF)]
    d = [zero, zero]
    for m in range(L):
        fields = [w_ref[0, x, m] for x in range(2)]
        sums = rows.around(*fields)
        for x in range(2):
            inverse = 1.0 / w_ref[2, x, m]
            a1, a2 = inverse * w_ref[1, x, m], inverse * w_ref[3, x, m]
            c_ref[0, x, m] = inverse
            c_ref[1, x, m] = a1
            c_ref[2, x, m] = a2
            f = forcing(fields[x], sums[x], inverse, a1, a2, shift[0])
            for h in range(HALF):
                g, rest[h][x] = factor(inverse, shift[h], rest[h][x])
                g_ref[h, x, m] = g
                if h == 0:
                    d[x] = g * (d[x] + f)
                    d_ref[x, m] = d[x]
    for x in range(2):
        for h in range(HALF):
            p, e = rest[h][x]
            rest_ref[2 * h + x] = e / p


def edge_rest_kernel(g_ref, c_ref, d_in, rest_ref, ish, pay, out, back, d_ref, f_ref):
    rows = Rows()
    lane = lanes()
    side = zone_side()
    zero = jnp.zeros((ROWS, COLS), F32)
    for i in range(8):
        back[i] = pay[i]
    d = [d_in[x, L - 1] for x in range(2)]
    for h in range(HALF):
        source = d_in if h == 0 else d_ref
        rest = [rest_ref[2 * h + x] for x in range(2)]
        up = [meet(d[x], rest[x], roll(d[x], 64), roll(rest[x], 64)) for x in range(2)]
        if h == HALF - 1:
            acc = zero
            for m in range(L - 1, -1, -1):
                up = [source[x, m] + g_ref[h, x, m] * up[x] for x in range(2)]
                out[m] = up[0]
                at = 4 * (m % 32)
                acc = jnp.where(lane < at + 4, roll(up[1], at - 68 - 4 * side), acc)
                if m % 32 == 0:
                    back[8 + m // 32] = acc
            break
        for m in range(L - 1, -1, -1):
            up = [source[x, m] + g_ref[h, x, m] * up[x] for x in range(2)]
            sums = rows.around(*up)
            for x in range(2):
                inverse, a1, a2 = c_ref[0, x, m], c_ref[1, x, m], c_ref[2, x, m]
                f_ref[x, m] = forcing(up[x], sums[x], inverse, a1, a2, ish[h + 1])
        d = [zero, zero]
        for m in range(L):
            for x in range(2):
                d[x] = g_ref[h + 1, x, m] * (d[x] + f_ref[x, m])
                d_ref[x, m] = d[x]


def shape(*dims):
    return jax.ShapeDtypeStruct((*dims, ROWS, COLS), F32)


VMEM = pl.BlockSpec(memory_space=pltpu.VMEM)
HBM = pl.BlockSpec(memory_space=pltpu.HBM)


def call(body, outs, scratch=(), flops=1, specs=VMEM, out_spec=VMEM):
    def run(*args):
        return pl.pallas_call(
            body,
            out_shape=outs,
            in_specs=[specs] * len(args),
            out_specs=jax.tree.map(lambda _: out_spec, outs),
            scratch_shapes=[
                pltpu.VMEM(s.shape, s.dtype) if isinstance(s, jax.ShapeDtypeStruct) else s
                for s in scratch
            ],
            compiler_params=pltpu.CompilerParams(vmem_limit_bytes=16 * 1024 * 1024),
            cost_estimate=pl.CostEstimate(flops=flops, bytes_accessed=0, transcendentals=0),
        )(*args)

    return run


def side_pairs(size):
    pairs = []
    for x in range(2):
        for y in range(1, size):
            a, b = x * size + y - 1, (3 - x) * size + y
            pairs += [(a, b), (b, a)]
        lone = (x * size + size - 1, (3 - x) * size)
        pairs += [(i, i) for i in lone]
    return pairs


def on_device(initial_field, plane_coupling, line_coupling, source, shift_table, shift_index):
    size = lax.axis_size("gy")
    whole = shape(L)
    *own, ish, z_out = call(
        load_kernel,
        tuple(pltpu.VMEM(w.shape, F32) for w in (whole,) * 4 + (shape(HALF), shape(L // 4))),
        (
            pltpu.SMEM(shift_table.shape, F32),
            pltpu.SMEM(shift_index.shape, jnp.int32),
            pltpu.SemaphoreType.DMA((6,)),
        ),
        specs=HBM,
    )(
        *(
            pltpu.with_memory_space_constraint(a, pltpu.HBM)
            for a in (
                initial_field, plane_coupling, line_coupling, source, shift_table, shift_index
            )
        )
    )
    z_oth = lax.ppermute(z_out, ZX, CROSS)
    oth = [lax.ppermute(a, "gx", SWAP) for a in own]

    steps = (shape(HALF, 2, L), shape(3, 2, L), shape(2, L))
    g, c, d, rest, pay = call(first_kernel, (*steps, shape(2 * HALF), shape(22)))(*own, *oth, ish)
    far_rest = lax.ppermute(pay, ZX, CROSS)

    z_in = lax.ppermute(z_oth, "gx", SWAP)
    out_b = call(pack_side_kernel, shape(L // 4))(*oth, z_oth)
    in_b = lax.ppermute(out_b, ("gz", "gx", "gy"), side_pairs(size))
    b_oth = lax.ppermute(in_b, "gx", SWAP)

    d, pay = call(
        middle_kernel, (shape(2, L), shape(8)), (shape(2, L), shape(2, L))
    )(ish, g, c, d, rest, far_rest)
    local = call(edge_local_kernel, shape(4, 2, L))(*own, *oth, z_in, z_oth)
    eg, ec, ed, er = call(
        edge_first_kernel, (*steps, shape(2 * HALF)), (shape(4, 2, L),)
    )(local, in_b, b_oth, ish)
    edge, pay = call(
        edge_rest_kernel, (whole, shape(10)), (shape(2, L), shape(2, L))
    )(eg, ec, ed, er, ish, pay)
    far = lax.ppermute(pay, ZX, CROSS)
    return call(
        last_kernel,
        whole,
        (whole, shape(2, L), whole, pltpu.SemaphoreType.DMA((L // CHUNK,))),
        out_spec=HBM,
    )(ish, g, c, d, rest, far_rest, far, edge)


def solution(mesh):
    spec = P("gz", "gx", "gy")

    return jax.shard_map(
        on_device, mesh=mesh, in_specs=(spec,) * 4 + (P(), P()), out_specs=spec, check_vma=False
    )
```

time: 38.7 us -> 28.6 us (0.74)
  the two profiles are of different devices: /device:TPU:92 before, /device:TPU:99 now
where the time goes in v1:
time: 28.6 us; the launch traced here: 28.5 us
  Pallas kernels  10.4 us (36%)
  waiting for transfers between devices  9.32 us (33%)
  starting transfers between devices  8.64 us (30%)
    pallas_call x8, Pallas kernels, run(): pl.pallas_call(body, out_shape=outs, in_specs=[specs] * len(args), out_sp...  10.4 us
    ppermute x1, starting transfers between devices, on_device(): in_b = lax.ppermute(out_b, ('gz', 'gx', 'gy'), side_pairs(size))  5.69 us
    ppermute x1, waiting for transfers between devices, on_device(): z_oth = lax.ppermute(z_out, ZX, CROSS)  3.58 us
    ppermute x1, waiting for transfers between devices, on_device(): far = lax.ppermute(pay, ZX, CROSS)  3.14 us
    ppermute x1, waiting for transfers between devices, on_device(): in_b = lax.ppermute(out_b, ('gz', 'gx', 'gy'), side_pairs(size))  1.48 us
    ppermute x4, starting transfers between devices, on_device(): oth = [lax.ppermute(a, 'gx', SWAP) for a in own]  1.36 us
    ppermute x1, waiting for transfers between devices, on_device(): far_rest = lax.ppermute(pay, ZX, CROSS)  1.1 us
  transfers between devices with their start and end apart: 10, of which 4 were waited for; matrix products, arithmetic and copies ran while one was open for 0% of the time, Pallas kernels for 14%

profile of v1, /device:TPU:99, one launch (start us, length us, event | category | flops | bytes accessed | tf_op | source)
XLA Modules:
  0.0 28.5 jit_solution(16657372139541848979)
XLA Ops:
  0.0 1.6 %shard_map.64 = (f32[64,8,128]{2,1,0:T(8,128)S(1)}, f32[64,8,128]{2,1,0:T(8,128)S(1)}, f32[64,8,128]{2,1,0:T(8,128)S(1)}, f32[64,8,128]{2,1,0:T(8,128)S(1)}, f32...) custom-call(f32[64,8,128]{2,1,0:T(8,128)} %u_in.1, f32[64,8,128]{2,1,0:T(8,128)} %p_in.1, f32[64,8,128]{2,1,0:T(8,128)} %l_in.1, ...), custom_call_target="tpu_custom_call" | custom-call | flops 1 | tf_op jit(solution)/shard_map/pallas_call | solution.py:383
  1.6 0.8 %collective-permute-start = (f32[64,8,128]{2,1,0:T(8,128)S(1)}, f32[64,8,128]{2,1,0:T(8,128)S(1)}, u32[]{:S(2)}, u32[]{:S(2)}) collective-permute-start(f32[64,8,128]{2,1,0:T(8,128)S(1)} %get-tuple-element.25.u), channel_id=1, source_target_pairs={{0,32},{32,0},{1,33},{33,1},{2,34},{34,2},{3,35},{35,3},{4,36},{36... | collective-permute-start | bytes 786440 | tf_op jit(solution)/shard_map/ppermute | solution.py:431
  2.3 0.1 collective-permute-start.1
  2.4 0.4 %collective-permute-start.2 = (f32[64,8,128]{2,1,0:T(8,128)S(1)}, f32[64,8,128]{2,1,0:T(8,128)S(1)}, u32[]{:S(2)}, u32[]{:S(2)}) collective-permute-start(f32[64,8,128]{2,1,0:T(8,128)S(1)} %get-tuple-element.27.l), channel_id=1, source_target_pairs={{0,32},{32,0},{1,33},{33,1},{2,34},{34,2},{3,35},{35,3},{4,36},{36... | collective-permute-start | bytes 786440 | tf_op jit(solution)/shard_map/ppermute | solution.py:431
  2.9 0.1 collective-permute-start.3
  3.0 0.6 %collective-permute-start.5 = (f32[16,8,128]{2,1,0:T(8,128)S(1)}, f32[16,8,128]{2,1,0:T(8,128)S(1)}, u32[]{:S(2)}, u32[]{:S(2)}) collective-permute-start(f32[16,8,128]{2,1,0:T(8,128)S(1)} %get-tuple-element.35), channel_id=1, source_target_pairs={{0,96},{32,64},{64,32},{96,0},{1,97},{33,65},{65,33},{97,1},{2,98}... | collective-permute-start | bytes 196616 | tf_op jit(solution)/shard_map/ppermute | solution.py:430
  3.5 3.6 %collective-permute-done.5.zo.z = f32[16,8,128]{2,1,0:T(8,128)S(1)} collective-permute-done((f32[16,8,128]{2,1,0:T(8,128)S(1)}, f32[16,8,128]{2,1,0:T(8,128)S(1)}, u32[]{:S(2)}, u32[]{:S(2)}) %collective-permute-start.5) | collective-permute-done | bytes 65568 | tf_op jit(solution)/shard_map/ppermute | solution.py:430
  7.1 0.0 collective-permute-done.uo.u
  7.1 0.0 collective-permute-done.1.po.p
  7.1 0.0 collective-permute-done.2.lo.l
  7.1 0.0 collective-permute-done.3.so.s
  7.1 0.6 %shard_map.68 = f32[16,8,128]{2,1,0:T(8,128)S(1)} custom-call(f32[64,8,128]{2,1,0:T(8,128)S(1)} %collective-permute-done.uo.u, f32[64,8,128]{2,1,0:T(8,128)S(1)} %collective-permute-done.1.po.p, f32[64,8,128]{2,1,0:T(8,128)S(1)} %collective-permute-done.2.lo.l, f32[64,8,128]{2,1,0:T(8,128)S(1)} %collective-permute-done.3.so.s, ...), custom_call_target="tpu_custom_call" | custom-call | flops 1 | tf_op jit(solution)/shard_map/pallas_call | solution.py:383
  7.8 5.7 %collective-permute-start.7 = (f32[16,8,128]{2,1,0:T(8,128)S(1)}, f32[16,8,128]{2,1,0:T(8,128)S(1)}, u32[]{:S(2)}, u32[]{:S(2)}) collective-permute-start(f32[16,8,128]{2,1,0:T(8,128)S(1)} %shard_map.68), channel_id=1, source_target_pairs={{0,97},{97,0},{1,98},{98,1},{2,99},{99,2},{3,100},{100,3},{4,101},... | collective-permute-start | bytes 196616 | tf_op jit(solution)/shard_map/ppermute | solution.py:439
  13.4 1.5 %shard_map.65 = (f32[4,2,64,8,128]{4,3,2,1,0:T(8,128)S(1)}, f32[3,2,64,8,128]{4,3,2,1,0:T(8,128)S(1)}, f32[2,64,8,128]{3,2,1,0:T(8,128)S(1)}, f32[8,8,128]{2,1,0:T(8,128)S(1)}, f32[22,8,128]{2,1,0:T(8,128)S(1)}) custom-call(f32[64,8,128]{2,1,0:T(8,128)S(1)} %get-tuple-element.25.u, f32[64,8,128]{2,1,0:T(8,128)S(1)} %get-tuple-element.26.p, ...), custom_call_target="tpu_custom_call" | custom-call | flops 1 | tf_op jit(solution)/shard_map/pallas_call | solution.py:383
  15.0 0.1 collective-permute-start.4
  15.1 0.2 collective-permute-start.6
  15.3 1.5 %collective-permute-done.7.b = f32[16,8,128]{2,1,0:T(8,128)S(1)} collective-permute-done((f32[16,8,128]{2,1,0:T(8,128)S(1)}, f32[16,8,128]{2,1,0:T(8,128)S(1)}, u32[]{:S(2)}, u32[]{:S(2)}) %collective-permute-start.7) | collective-permute-done | bytes 65568 | tf_op jit(solution)/shard_map/ppermute | solution.py:439
  16.8 0.4 %collective-permute-start.8 = (f32[16,8,128]{2,1,0:T(8,128)S(1)}, f32[16,8,128]{2,1,0:T(8,128)S(1)}, u32[]{:S(2)}, u32[]{:S(2)}) collective-permute-start(f32[16,8,128]{2,1,0:T(8,128)S(1)} %collective-permute-done.7.b), channel_id=1, source_target_pairs={{0,32},{32,0},{1,33},{33,1},{2,34},{34,2},{3,35},{35,3},{4,36},{36... | collective-permute-start | bytes 196616 | tf_op jit(solution)/shard_map/ppermute | solution.py:440
  17.1 0.0 collective-permute-done.6.z
  17.1 1.2 %shard_map.67.v_ref = f32[4,2,64,8,128]{4,3,2,1,0:T(8,128)S(1)} custom-call(f32[64,8,128]{2,1,0:T(8,128)S(1)} %get-tuple-element.25.u, f32[64,8,128]{2,1,0:T(8,128)S(1)} %get-tuple-element.26.p, f32[64,8,128]{2,1,0:T(8,128)S(1)} %get-tuple-element.27.l, f32[64,8,128]{2,1,0:T(8,128)S(1)} %get-tuple-element.28.s, f32[64,8,128]{2,1,0:T(8,128)S(1)} %collective-permute-done.uo.u, ...), custom_call_target="tpu_custom_call" | custom-call | flops 1 | tf_op jit(solution)/shard_map/pallas_call | solution.py:383
  18.3 1.1 %collective-permute-done.4.far.far_rest = f32[22,8,128]{2,1,0:T(8,128)S(1)} collective-permute-done((f32[22,8,128]{2,1,0:T(8,128)S(1)}, f32[22,8,128]{2,1,0:T(8,128)S(1)}, u32[]{:S(2)}, u32[]{:S(2)}) %collective-permute-start.4) | collective-permute-done | bytes 90144 | tf_op jit(solution)/shard_map/ppermute | solution.py:435
  19.4 1.3 %shard_map.66 = (f32[2,64,8,128]{3,2,1,0:T(8,128)S(1)}, f32[8,8,128]{2,1,0:T(8,128)S(1)}) custom-call(f32[4,8,128]{2,1,0:T(8,128)S(1)} %get-tuple-element.24.ish, f32[4,2,64,8,128]{4,3,2,1,0:T(8,128)S(1)} %get-tuple-element.29.g, f32[3,2,64,8,128]{4,3,2,1,0:T(8,128)S(1)} %get-tuple-element.30.c, f32[2,64,8,128]{3,2,1,0:T(8,128)S(1)} %get-tuple-element.31.d, ...), custom_call_target="tpu_custom_call" | custom-call | flops 1 | tf_op jit(solution)/shard_map/pallas_call | solution.py:383
  20.7 0.0 collective-permute-done.8.bo
  20.7 1.1 %shard_map.69 = (f32[4,2,64,8,128]{4,3,2,1,0:T(8,128)S(1)}, f32[3,2,64,8,128]{4,3,2,1,0:T(8,128)S(1)}, f32[2,64,8,128]{3,2,1,0:T(8,128)S(1)}, f32[8,8,128]{2,1,0:T(8,128)S(1)}) custom-call(f32[4,2,64,8,128]{4,3,2,1,0:T(8,128)S(1)} %shard_map.67.v_ref, f32[16,8,128]{2,1,0:T(8,128)S(1)} %collective-permute-done.7.b, ...), custom_call_target="tpu_custom_call" | custom-call | flops 1 | tf_op jit(solution)/shard_map/pallas_call | solution.py:383
  21.9 1.9 %shard_map.70 = (f32[64,8,128]{2,1,0:T(8,128)S(1)}, f32[10,8,128]{2,1,0:T(8,128)S(1)}) custom-call(f32[4,2,64,8,128]{4,3,2,1,0:T(8,128)S(1)} %get-tuple-element.36.g_ref, f32[3,2,64,8,128]{4,3,2,1,0:T(8,128)S(1)} %get-tuple-element.37.c_ref, f32[2,64,8,128]{3,2,1,0:T(8,128)S(1)} %get-tuple-element.38.d_in, f32[8,8,128]{2,1,0:T(8,128)S(1)} %get-tuple-element.39.rest_ref, ...), custom_call_target="tpu_custom_call" | custom-call | flops 1 | tf_op jit(solution)/shard_map/pallas_call | solution.py:383
  23.8 0.4 %collective-permute-start.9 = (f32[10,8,128]{2,1,0:T(8,128)S(1)}, f32[10,8,128]{2,1,0:T(8,128)S(1)}, u32[]{:S(2)}, u32[]{:S(2)}) collective-permute-start(f32[10,8,128]{2,1,0:T(8,128)S(1)} %get-tuple-element.41), channel_id=1, source_target_pairs={{0,96},{32,64},{64,32},{96,0},{1,97},{33,65},{65,33},{97,1},{2,98}... | collective-permute-start | bytes 122888 | tf_op jit(solution)/shard_map/ppermute | solution.py:452
  24.2 3.1 %collective-permute-done.9.far = f32[10,8,128]{2,1,0:T(8,128)S(1)} collective-permute-done((f32[10,8,128]{2,1,0:T(8,128)S(1)}, f32[10,8,128]{2,1,0:T(8,128)S(1)}, u32[]{:S(2)}, u32[]{:S(2)}) %collective-permute-start.9) | collective-permute-done | bytes 40992 | tf_op jit(solution)/shard_map/ppermute | solution.py:452
  27.3 1.2 %shard_map.71 = f32[64,8,128]{2,1,0:T(8,128)} custom-call(f32[4,8,128]{2,1,0:T(8,128)S(1)} %get-tuple-element.24.ish, f32[4,2,64,8,128]{4,3,2,1,0:T(8,128)S(1)} %get-tuple-element.29.g, f32[3,2,64,8,128]{4,3,2,1,0:T(8,128)S(1)} %get-tuple-element.30.c, f32[2,64,8,128]{3,2,1,0:T(8,128)S(1)} %get-tuple-element.34.d, f32[8,8,128]{2,1,0:T(8,128)S(1)} %get-tuple-element.32.rest, ...), custom_call_target="tpu_custom_call" | custom-call | flops 1 | tf_op jit(solution)/shard_map/pallas_call | solution.py:383
Async XLA Ops:
  1.6 5.5 %collective-permute-start = (f32[64,8,128]{2,1,0:T(8,128)S(1)}, f32[64,8,128]{2,1,0:T(8,128)S(1)}, u32[]{:S(2)}, u32[]{:S(2)}) collective-permute-start(f32[64,8,128]{2,1,0:T(8,128)S(1)} %get-tuple-element.25.u), channel_id=1, source_target_pairs={{0,32},{32,0},{1,33},{33,1},{2,34},{34,2},{3,35},{35,3},{4,36},{36... | collective-permute-start | bytes 786440 | tf_op jit(solution)/shard_map/ppermute | solution.py:431
  2.3 4.8 %collective-permute-start.1 = (f32[64,8,128]{2,1,0:T(8,128)S(1)}, f32[64,8,128]{2,1,0:T(8,128)S(1)}, u32[]{:S(2)}, u32[]{:S(2)}) collective-permute-start(f32[64,8,128]{2,1,0:T(8,128)S(1)} %get-tuple-element.26.p), channel_id=1, source_target_pairs={{0,32},{32,0},{1,33},{33,1},{2,34},{34,2},{3,35},{35,3},{4,36},{36... | collective-permute-start | bytes 786440 | tf_op jit(solution)/shard_map/ppermute | solution.py:431
  2.4 4.7 %collective-permute-start.2 = (f32[64,8,128]{2,1,0:T(8,128)S(1)}, f32[64,8,128]{2,1,0:T(8,128)S(1)}, u32[]{:S(2)}, u32[]{:S(2)}) collective-permute-start(f32[64,8,128]{2,1,0:T(8,128)S(1)} %get-tuple-element.27.l), channel_id=1, source_target_pairs={{0,32},{32,0},{1,33},{33,1},{2,34},{34,2},{3,35},{35,3},{4,36},{36... | collective-permute-start | bytes 786440 | tf_op jit(solution)/shard_map/ppermute | solution.py:431
  2.9 4.3 %collective-permute-start.3 = (f32[64,8,128]{2,1,0:T(8,128)S(1)}, f32[64,8,128]{2,1,0:T(8,128)S(1)}, u32[]{:S(2)}, u32[]{:S(2)}) collective-permute-start(f32[64,8,128]{2,1,0:T(8,128)S(1)} %get-tuple-element.28.s), channel_id=1, source_target_pairs={{0,32},{32,0},{1,33},{33,1},{2,34},{34,2},{3,35},{35,3},{4,36},{36... | collective-permute-start | bytes 786440 | tf_op jit(solution)/shard_map/ppermute | solution.py:431
  3.0 4.1 %collective-permute-start.5 = (f32[16,8,128]{2,1,0:T(8,128)S(1)}, f32[16,8,128]{2,1,0:T(8,128)S(1)}, u32[]{:S(2)}, u32[]{:S(2)}) collective-permute-start(f32[16,8,128]{2,1,0:T(8,128)S(1)} %get-tuple-element.35), channel_id=1, source_target_pairs={{0,96},{32,64},{64,32},{96,0},{1,97},{33,65},{65,33},{97,1},{2,98}... | collective-permute-start | bytes 196616 | tf_op jit(solution)/shard_map/ppermute | solution.py:430
  7.8 9.0 %collective-permute-start.7 = (f32[16,8,128]{2,1,0:T(8,128)S(1)}, f32[16,8,128]{2,1,0:T(8,128)S(1)}, u32[]{:S(2)}, u32[]{:S(2)}) collective-permute-start(f32[16,8,128]{2,1,0:T(8,128)S(1)} %shard_map.68), channel_id=1, source_target_pairs={{0,97},{97,0},{1,98},{98,1},{2,99},{99,2},{3,100},{100,3},{4,101},... | collective-permute-start | bytes 196616 | tf_op jit(solution)/shard_map/ppermute | solution.py:439
  15.0 4.4 %collective-permute-start.4 = (f32[22,8,128]{2,1,0:T(8,128)S(1)}, f32[22,8,128]{2,1,0:T(8,128)S(1)}, u32[]{:S(2)}, u32[]{:S(2)}) collective-permute-start(f32[22,8,128]{2,1,0:T(8,128)S(1)} %get-tuple-element.33), channel_id=1, source_target_pairs={{0,96},{32,64},{64,32},{96,0},{1,97},{33,65},{65,33},{97,1},{2,98}... | collective-permute-start | bytes 270344 | tf_op jit(solution)/shard_map/ppermute | solution.py:435
  15.1 2.1 %collective-permute-start.6 = (f32[16,8,128]{2,1,0:T(8,128)S(1)}, f32[16,8,128]{2,1,0:T(8,128)S(1)}, u32[]{:S(2)}, u32[]{:S(2)}) collective-permute-start(f32[16,8,128]{2,1,0:T(8,128)S(1)} %collective-permute-done.5.zo.z), channel_id=1, source_target_pairs={{0,32},{32,0},{1,33},{33,1},{2,34},{34,2},{3,35},{35,3},{4,36},{36... | collective-permute-start | bytes 196616 | tf_op jit(solution)/shard_map/ppermute | solution.py:437
  16.8 4.0 %collective-permute-start.8 = (f32[16,8,128]{2,1,0:T(8,128)S(1)}, f32[16,8,128]{2,1,0:T(8,128)S(1)}, u32[]{:S(2)}, u32[]{:S(2)}) collective-permute-start(f32[16,8,128]{2,1,0:T(8,128)S(1)} %collective-permute-done.7.b), channel_id=1, source_target_pairs={{0,32},{32,0},{1,33},{33,1},{2,34},{34,2},{3,35},{35,3},{4,36},{36... | collective-permute-start | bytes 196616 | tf_op jit(solution)/shard_map/ppermute | solution.py:440
  23.8 3.5 %collective-permute-start.9 = (f32[10,8,128]{2,1,0:T(8,128)S(1)}, f32[10,8,128]{2,1,0:T(8,128)S(1)}, u32[]{:S(2)}, u32[]{:S(2)}) collective-permute-start(f32[10,8,128]{2,1,0:T(8,128)S(1)} %get-tuple-element.41), channel_id=1, source_target_pairs={{0,96},{32,64},{64,32},{96,0},{1,97},{33,65},{65,33},{97,1},{2,98}... | collective-permute-start | bytes 122888 | tf_op jit(solution)/shard_map/ppermute | solution.py:452

commit v2 on v1

--- a/solution.py
+++ b/solution.py
@@ -144,18 +144,16 @@
     copies[4].wait()
     for h in range(HALF):
         ish[h] = 1.0 / jnp.full((ROWS, COLS), table[index[h]], F32)
-    for copy in copies[:4]:
-        copy.wait()
     side = zone_side()
-    for q in range(L // 4):
-        acc = None
-        for i in range(4):
-            k = layer(4 * q + i)
-            for a, ref in enumerate((u, p, l, s)):
-                at = 32 * i + 8 * a
-                piece = roll(ref[k], at + 8 * (1 - side))
-                acc = piece if acc is None else jnp.where(lane >= at, piece, acc)
-        out[q] = acc
+    for a, ref in enumerate((u, p, l, s)):
+        copies[a].wait()
+        mine = (lane // 8) % 4 == a
+        for q in range(L // 4):
+            acc = None
+            for i in range(4):
+                piece = roll(ref[layer(4 * q + i)], 32 * i + 8 * a + 8 * (1 - side))
+                acc = piece if acc is None else jnp.where(lane >= 32 * i, piece, acc)
+            out[q] = acc if a == 0 else jnp.where(mine, acc, out[q])
 
 
 def pack_side_kernel(u, p, l, s, z, out):
@@ -163,24 +161,26 @@
     side = zone_side()
     for q in range(L // 4):
         acc = None
-        for half in range(2):
-            for i in range(4):
-                for a, ref in enumerate((u, p, l, s)):
-                    at = 64 * half + 16 * i + 4 * a
-                    if half == 0:
-                        piece = roll(z[q], at - (32 * i + 8 * a) - 4 * side)
-                    else:
-                        piece = roll(ref[layer(4 * q + i)], at + 4 * side)
-                    acc = piece if acc is None else jnp.where(lane >= at, piece, acc)
+        for pair in range(2):
+            for half in range(2):
+                for odd in range(2):
+                    i = 2 * pair + odd
+                    for a, ref in enumerate((u, p, l, s)):
+                        at = 64 * pair + 32 * half + 16 * odd + 4 * a
+                        if half == 0:
+                            piece = roll(z[q], at - (32 * i + 8 * a) - 4 * side)
+                        else:
+                            piece = roll(ref[layer(4 * q + i)], at + 4 * side)
+                        acc = piece if acc is None else jnp.where(lane >= at, piece, acc)
         out[q] = acc
 
 
 def first_kernel(u, p, l, s, uo, po, lo, so, ish, g_out, c_out, d_out, rest_out, pay):
     rows = Rows()
-    shift = [ish[h] for h in range(HALF)]
+    shift = [ish[h] for h in range(2)]
     one = jnp.full((ROWS, COLS), 1.0, F32)
     zero = jnp.zeros((ROWS, COLS), F32)
-    rest = [[(one, one)] * 2 for _ in range(HALF)]
+    rest = [[(one, one)] * 2 for _ in range(2)]
     d = [zero, zero]
     for m in range(L):
         k = layer(m)
@@ -193,7 +193,7 @@
             c_out[1, x, m] = a1
             c_out[2, x, m] = a2
             f = forcing(fields[x], sums[x], inverse, a1, a2, shift[0])
-            for h in range(HALF):
+            for h in range(2):
                 g, rest[h][x] = factor(inverse, shift[h], rest[h][x])
                 g_out[h, x, m] = g
                 if h == 0:
@@ -202,15 +202,15 @@
     total = reach(0, rows, shift[1], g_out, c_out, d_out, (0, 1))
     for x in range(2):
         pay[x] = d[x]
-        for h in range(HALF):
+        for h in range(2):
             p, e = rest[h][x]
             rest_out[2 * h + x] = e / p
             pay[2 + 2 * h + x] = e / p
         for i in range(6):
-            pay[10 + 6 * x + i] = total[x][i]
-
-
-def middle_kernel(ish, g, c, d, rest, far, d_out, pay, f_ref, d_ref):
+            pay[6 + 6 * x + i] = total[x][i]
+
+
+def middle_kernel(ish, g, c, d, rest, far, g_out, d_out, rest_out, pay, f_ref, d_ref):
     rows = Rows()
     zero = jnp.zeros((ROWS, COLS), F32)
 
@@ -223,12 +223,16 @@
         if m == L - 1:
             last = up
         explicit(rows, up, c, m, ish[1], f_ref)
+    one = jnp.full((ROWS, COLS), 1.0, F32)
+    after = [[(one, one)] * 2 for _ in range(2)]
     now = [zero, zero]
     for m in range(L):
         for x in range(2):
+            for h in range(2):
+                g_out[h, x, m], after[h][x] = factor(c[0, x, m], ish[2 + h], after[h][x])
             now[x] = g[1, x, m] * (now[x] + f_ref[x, m])
             d_ref[x, m] = now[x]
-    far_d = reached(rows, [lambda i, x=x: far[10 + 6 * (1 - x) + i] for x in range(2)], last)
+    far_d = reached(rows, [lambda i, x=x: far[6 + 6 * (1 - x) + i] for x in range(2)], last)
     up = [meet(now[x], rest[2 + x], far_d[x], far_rest(1, x)) for x in range(2)]
     for m in range(L - 1, -1, -1):
         up = [d_ref[x, m] + g[1, x, m] * up[x] for x in range(2)]
@@ -236,42 +240,54 @@
     now = [zero, zero]
     for m in range(L):
         for x in range(2):
-            now[x] = g[2, x, m] * (now[x] + f_ref[x, m])
+            now[x] = g_out[0, x, m] * (now[x] + f_ref[x, m])
             d_out[x, m] = now[x]
-    total = reach(2, rows, ish[3], g, c, d_out, (1,))
+    total = reach(0, rows, ish[3], g_out, c, d_out, (1,))
     for x in range(2):
         pay[x] = now[x]
+        for h in range(2):
+            p, e = after[h][x]
+            rest_out[2 * h + x] = e / p
+            pay[8 + 2 * h + x] = e / p
     for i in range(6):
         pay[2 + i] = total[1][i]
 
 
-def last_kernel(ish, g, c, d, rest, far_rest, far, edge, out, field, f_ref, d_ref, sem):
+def own_columns(side):
     lane = lanes()
+    zone = (COLS - 4) * side
+    return (lane >= zone) & (lane < zone + 4)
+
+
+def finish_kernel(ish, g, c, d, rest, far, edge, out, f_ref, d_ref):
     rows = Rows()
-    gz = lax.axis_index("gz")
     side = zone_side()
-    up = [meet(d[x, L - 1], rest[4 + x], far[1 - x], far_rest[6 + 1 - x]) for x in range(2)]
+    here = own_columns(side)
+    up = [meet(d[x, L - 1], rest[x], far[1 - x], far[8 + 1 - x]) for x in range(2)]
     for m in range(L - 1, -1, -1):
-        up = [d[x, m] + g[2, x, m] * up[x] for x in range(2)]
+        up = [d[x, m] + g[0, x, m] * up[x] for x in range(2)]
         if m == L - 1:
             last = up
         explicit(rows, up, c, m, ish[3], f_ref, (0,))
     now = jnp.zeros((ROWS, COLS), F32)
     for m in range(L):
-        now = g[3, 0, m] * (now + f_ref[0, m])
+        now = g[1, 0, m] * (now + f_ref[0, m])
         d_ref[m] = now
     far_d = reached(rows, [lambda i: far[2 + i], None], last)[0]
-    up = meet(now, rest[6], far_d, far_rest[8 + 1])
-    zone = jnp.where(side == 0, 0, COLS - 4)
-    here = (lane >= zone) & (lane < zone + 4)
-    other = COLS - 4 - zone
-    there = (lane >= other) & (lane < other + 4)
+    up = meet(now, rest[2], far_d, far[10 + 1])
+    for m in range(L - 1, -1, -1):
+        up = d_ref[m] + g[1, 0, m] * up
+        out[layer(m)] = jnp.where(here, roll(edge[m], -4 + 120 * side), up)
+
+
+def last_kernel(value, far, out, field, sem):
+    gz = lax.axis_index("gz")
+    other = 1 - zone_side()
+    there = own_columns(other)
     copies = []
     for m in range(L - 1, -1, -1):
-        up = d_ref[m] + g[HALF - 1, 0, m] * up
-        v = jnp.where(here, roll(edge[m], -4 + 120 * side), up)
-        got = roll(far[8 + m // 32], other - 4 * (m % 32))
-        field[layer(m)] = jnp.where(there, got, v)
+        got = roll(far[m // 32], (COLS - 4) * other - 4 * (m % 32))
+        field[layer(m)] = jnp.where(there, got, value[layer(m)])
         if m % CHUNK == 0:
             start = jnp.where(gz == 0, m, L - CHUNK - m)
             part = pl.ds(start, CHUNK)
@@ -281,23 +297,51 @@
         copy.wait()
 
 
-def edge_local_kernel(u, p, l, s, uo, po, lo, so, z, zo, out):
+class Groups:
+    def __init__(self):
+        gx = lax.axis_index("gx")
+        lane, sub = lanes(), subs()
+        self.own = lane < 64
+        self.near = lax.rem(lane, 64) < 32
+        self.top = sub == 0
+        self.bottom = sub == ROWS - 1
+        low = jnp.where(gx == 0, 1.0, 0.0).astype(F32)
+        self.before = jnp.where(self.own, 1.0 - low, low)
+        self.after = jnp.where(self.own, low, 1.0 - low)
+
+    def around(self, v):
+        a, c = pltpu.roll(v, 1, 0), pltpu.roll(v, ROWS - 1, 0)
+        across = roll(jnp.where(self.top, a, c), 64)
+        before = jnp.where(self.top, self.before * across, a)
+        after = jnp.where(self.bottom, self.after * across, c)
+        return (before + after) + (roll(v, 1) + roll(v, -1))
+
+    def far(self, v):
+        return jnp.where(self.near, roll(v, -32), roll(v, 32))
+
+
+def edge_local_kernel(u, p, l, s, uo, po, lo, so, z, zo, out, packed):
     side = zone_side()
-    far = lanes() >= 64
+    lane = lanes()
+    near = lax.rem(lane, 64) < 32
+    own = lane < 64
+    for q in range(L // 4):
+        across = roll(zo[q], 64)
+        for i in range(4):
+            packed[4 * q + i] = jnp.where(lane // 32 == i, z[q], across)
     for m in range(L):
         k = layer(m)
-        for x, refs in enumerate(((u, p, l, s, z), (uo, po, lo, so, zo))):
-            for a in range(4):
-                near = roll(refs[a][k], 4 + 8 * side)
-                beyond = roll(refs[4][m // 4], 68 - 32 * (m % 4) - 8 * a)
-                out[a, x, m] = jnp.where(far, beyond, near)
-
-
-def edge_first_kernel(v_ref, b, bo, ish, g_ref, c_ref, d_ref, rest_ref, w_ref):
-    rows = Rows()
+        for a, (ref, other) in enumerate(zip((u, p, l, s), (uo, po, lo, so))):
+            here = jnp.where(own, roll(ref[k], 4 + 8 * side), roll(other[k], 68 + 8 * side))
+            there = roll(packed[m], 36 - 32 * (m % 4) - 8 * a)
+            out[a, m] = jnp.where(near, here, there)
+
+
+def edge_first_kernel(v_ref, b, bo, ish, g_ref, c_ref, d_ref, rest_ref, w_ref, pairs, f_ref):
+    groups = Groups()
     side = zone_side()
     gy = lax.axis_index("gy")
-    within = lax.rem(lanes(), 64)
+    within = lax.rem(lanes(), 32)
     inner = (within >= 4) & (within < 12)
     zone = 12 * side
     halo = (within >= zone) & (within < zone + 4)
@@ -306,68 +350,65 @@
     shift = [ish[h] for h in range(HALF)]
     one = jnp.full((ROWS, COLS), 1.0, F32)
     zero = jnp.zeros((ROWS, COLS), F32)
-    for m in range(L):
-        for x, ref in enumerate((b, bo)):
-            for a in range(4):
-                v = jnp.where(halo, roll(ref[m // 4], zone - 16 * (m % 4) - 4 * a), v_ref[a, x, m])
-                w_ref[a, x, m] = jnp.where(keep, v, 1000.0 * one if a == 2 else zero)
-    rest = [[(one, one)] * 2 for _ in range(HALF)]
-    d = [zero, zero]
-    for m in range(L):
-        fields = [w_ref[0, x, m] for x in range(2)]
-        sums = rows.around(*fields)
-        for x in range(2):
-            inverse = 1.0 / w_ref[2, x, m]
-            a1, a2 = inverse * w_ref[1, x, m], inverse * w_ref[3, x, m]
-            c_ref[0, x, m] = inverse
-            c_ref[1, x, m] = a1
-            c_ref[2, x, m] = a2
-            f = forcing(fields[x], sums[x], inverse, a1, a2, shift[0])
-            for h in range(HALF):
-                g, rest[h][x] = factor(inverse, shift[h], rest[h][x])
-                g_ref[h, x, m] = g
-                if h == 0:
-                    d[x] = g * (d[x] + f)
-                    d_ref[x, m] = d[x]
-    for x in range(2):
+    for q in range(L // 4):
+        pairs[2 * q] = jnp.where(groups.own, b[q], roll(bo[q], 64))
+        pairs[2 * q + 1] = jnp.where(groups.own, roll(b[q], 64), bo[q])
+    for m in range(L):
+        for a in range(4):
+            side_columns = roll(pairs[m // 2], zone - 16 * (m % 2) - 4 * a)
+            v = jnp.where(halo, side_columns, v_ref[a, m])
+            w_ref[a, m] = jnp.where(keep, v, 1000.0 * one if a == 2 else zero)
+    rest = [(one, one)] * HALF
+    d = zero
+    for m in range(L):
+        field = w_ref[0, m]
+        inverse = 1.0 / w_ref[2, m]
+        a1, a2 = inverse * w_ref[1, m], inverse * w_ref[3, m]
+        c_ref[0, m] = inverse
+        c_ref[1, m] = a1
+        c_ref[2, m] = a2
+        f_ref[m] = forcing(field, groups.around(field), inverse, a1, a2, shift[0])
+    for m in range(L):
         for h in range(HALF):
-            p, e = rest[h][x]
-            rest_ref[2 * h + x] = e / p
-
-
-def edge_rest_kernel(g_ref, c_ref, d_in, rest_ref, ish, pay, out, back, d_ref, f_ref):
-    rows = Rows()
+            g, rest[h] = factor(c_ref[0, m], shift[h], rest[h])
+            g_ref[h, m] = g
+            if h == 0:
+                d = g * (d + f_ref[m])
+                d_ref[m] = d
+    for h in range(HALF):
+        p, e = rest[h]
+        rest_ref[h] = e / p
+
+
+def edge_rest_kernel(g_ref, c_ref, d_in, rest_ref, ish, out, back, d_ref, f_ref):
+    groups = Groups()
     lane = lanes()
     side = zone_side()
     zero = jnp.zeros((ROWS, COLS), F32)
-    for i in range(8):
-        back[i] = pay[i]
-    d = [d_in[x, L - 1] for x in range(2)]
+    d = d_in[L - 1]
     for h in range(HALF):
         source = d_in if h == 0 else d_ref
-        rest = [rest_ref[2 * h + x] for x in range(2)]
-        up = [meet(d[x], rest[x], roll(d[x], 64), roll(rest[x], 64)) for x in range(2)]
+        rest = rest_ref[h]
+        up = meet(d, rest, groups.far(d), groups.far(rest))
         if h == HALF - 1:
             acc = zero
             for m in range(L - 1, -1, -1):
-                up = [source[x, m] + g_ref[h, x, m] * up[x] for x in range(2)]
-                out[m] = up[0]
+                up = source[m] + g_ref[h, m] * up
+                out[m] = up
                 at = 4 * (m % 32)
-                acc = jnp.where(lane < at + 4, roll(up[1], at - 68 - 4 * side), acc)
+                acc = jnp.where(lane < at + 4, roll(up, at - 100 - 4 * side), acc)
                 if m % 32 == 0:
-                    back[8 + m // 32] = acc
+                    back[m // 32] = acc
             break
         for m in range(L - 1, -1, -1):
-            up = [source[x, m] + g_ref[h, x, m] * up[x] for x in range(2)]
-            sums = rows.around(*up)
-            for x in range(2):
-                inverse, a1, a2 = c_ref[0, x, m], c_ref[1, x, m], c_ref[2, x, m]
-                f_ref[x, m] = forcing(up[x], sums[x], inverse, a1, a2, ish[h + 1])
-        d = [zero, zero]
+            up = source[m] + g_ref[h, m] * up
+            f_ref[m] = forcing(
+                up, groups.around(up), c_ref[0, m], c_ref[1, m], c_ref[2, m], ish[h + 1]
+            )
+        d = zero
         for m in range(L):
-            for x in range(2):
-                d[x] = g_ref[h + 1, x, m] * (d[x] + f_ref[x, m])
-                d_ref[x, m] = d[x]
+            d = g_ref[h + 1, m] * (d + f_ref[m])
+            d_ref[m] = d
 
 
 def shape(*dims):
@@ -430,32 +471,34 @@
     z_oth = lax.ppermute(z_out, ZX, CROSS)
     oth = [lax.ppermute(a, "gx", SWAP) for a in own]
 
-    steps = (shape(HALF, 2, L), shape(3, 2, L), shape(2, L))
-    g, c, d, rest, pay = call(first_kernel, (*steps, shape(2 * HALF), shape(22)))(*own, *oth, ish)
-    far_rest = lax.ppermute(pay, ZX, CROSS)
+    g, c, d, rest, pay = call(
+        first_kernel, (shape(2, 2, L), shape(3, 2, L), shape(2, L), shape(4), shape(18))
+    )(*own, *oth, ish)
+    far = lax.ppermute(pay, ZX, CROSS)
 
     z_in = lax.ppermute(z_oth, "gx", SWAP)
     out_b = call(pack_side_kernel, shape(L // 4))(*oth, z_oth)
     in_b = lax.ppermute(out_b, ("gz", "gx", "gy"), side_pairs(size))
     b_oth = lax.ppermute(in_b, "gx", SWAP)
 
-    d, pay = call(
-        middle_kernel, (shape(2, L), shape(8)), (shape(2, L), shape(2, L))
-    )(ish, g, c, d, rest, far_rest)
-    local = call(edge_local_kernel, shape(4, 2, L))(*own, *oth, z_in, z_oth)
+    g, d, rest, pay = call(
+        middle_kernel,
+        (shape(2, 2, L), shape(2, L), shape(4), shape(12)),
+        (shape(2, L), shape(2, L)),
+    )(ish, g, c, d, rest, far)
+    far = lax.ppermute(pay, ZX, CROSS)
+    local = call(edge_local_kernel, shape(4, L), (whole,))(*own, *oth, z_in, z_oth)
     eg, ec, ed, er = call(
-        edge_first_kernel, (*steps, shape(2 * HALF)), (shape(4, 2, L),)
+        edge_first_kernel,
+        (shape(HALF, L), shape(3, L), whole, shape(HALF)),
+        (shape(4, L), shape(L // 2), whole),
     )(local, in_b, b_oth, ish)
-    edge, pay = call(
-        edge_rest_kernel, (whole, shape(10)), (shape(2, L), shape(2, L))
-    )(eg, ec, ed, er, ish, pay)
-    far = lax.ppermute(pay, ZX, CROSS)
+    edge, back = call(edge_rest_kernel, (whole, shape(2)), (whole, whole))(eg, ec, ed, er, ish)
+    back = lax.ppermute(back, ZX, CROSS)
+    value = call(finish_kernel, whole, (shape(1, L), whole))(ish, g, c, d, rest, far, edge)
     return call(
-        last_kernel,
-        whole,
-        (whole, shape(2, L), whole, pltpu.SemaphoreType.DMA((L // CHUNK,))),
-        out_spec=HBM,
-    )(ish, g, c, d, rest, far_rest, far, edge)
+        last_kernel, whole, (whole, pltpu.SemaphoreType.DMA((L // CHUNK,))), out_spec=HBM
+    )(value, back)
 
 
 def solution(mesh):

time: 28.6 us -> 29.2 us (1.021)
  the two profiles are of different devices: /device:TPU:99 before, /device:TPU:97 now
where the time goes in v2:
time: 29.2 us; the launch traced here: 29 us
  starting transfers between devices  12.3 us (42%)
  Pallas kernels  9.73 us (33%)
  waiting for transfers between devices  6.93 us (24%)
    pallas_call x9, Pallas kernels, run(): pl.pallas_call(body, out_shape=outs, in_specs=[specs] * len(args), out_sp...  9.73 us
    ppermute x1, starting transfers between devices, on_device(): in_b = lax.ppermute(out_b, ('gz', 'gx', 'gy'), side_pairs(size))  4.67 us
    ppermute x2, starting transfers between devices, on_device(): far = lax.ppermute(pay, ZX, CROSS)  3.86 us
    ppermute x1, waiting for transfers between devices, on_device(): z_oth = lax.ppermute(z_out, ZX, CROSS)  2.63 us
    ppermute x1, waiting for transfers between devices, on_device(): back = lax.ppermute(back, ZX, CROSS)  2.26 us
    ppermute x2, waiting for transfers between devices, on_device(): far = lax.ppermute(pay, ZX, CROSS)  2.02 us
    ppermute x1, starting transfers between devices, on_device(): z_oth = lax.ppermute(z_out, ZX, CROSS)  1.51 us
    ppermute x4, starting transfers between devices, on_device(): oth = [lax.ppermute(a, 'gx', SWAP) for a in own]  1.36 us
  transfers between devices with their start and end apart: 11, of which 3 were waited for; matrix products, arithmetic and copies ran while one was open for 0% of the time, Pallas kernels for 24%

profile of v2, /device:TPU:97, one launch (start us, length us, event | category | flops | bytes accessed | tf_op | source)
XLA Modules:
  0.0 29.0 jit_solution(444537998100439129)
XLA Ops:
  0.0 1.6 %shard_map.64 = (f32[64,8,128]{2,1,0:T(8,128)S(1)}, f32[64,8,128]{2,1,0:T(8,128)S(1)}, f32[64,8,128]{2,1,0:T(8,128)S(1)}, f32[64,8,128]{2,1,0:T(8,128)S(1)}, f32...) custom-call(f32[64,8,128]{2,1,0:T(8,128)} %u_in.1, f32[64,8,128]{2,1,0:T(8,128)} %p_in.1, f32[64,8,128]{2,1,0:T(8,128)} %l_in.1, ...), custom_call_target="tpu_custom_call" | custom-call | flops 1 | tf_op jit(solution)/shard_map/pallas_call | solution.py:424
  1.6 0.8 %collective-permute-start = (f32[64,8,128]{2,1,0:T(8,128)S(1)}, f32[64,8,128]{2,1,0:T(8,128)S(1)}, u32[]{:S(2)}, u32[]{:S(2)}) collective-permute-start(f32[64,8,128]{2,1,0:T(8,128)S(1)} %get-tuple-element.27.u), channel_id=1, source_target_pairs={{0,32},{32,0},{1,33},{33,1},{2,34},{34,2},{3,35},{35,3},{4,36},{36... | collective-permute-start | bytes 786440 | tf_op jit(solution)/shard_map/ppermute | solution.py:472
  2.3 0.1 collective-permute-start.1
  2.4 0.4 %collective-permute-start.2 = (f32[64,8,128]{2,1,0:T(8,128)S(1)}, f32[64,8,128]{2,1,0:T(8,128)S(1)}, u32[]{:S(2)}, u32[]{:S(2)}) collective-permute-start(f32[64,8,128]{2,1,0:T(8,128)S(1)} %get-tuple-element.29.l), channel_id=1, source_target_pairs={{0,32},{32,0},{1,33},{33,1},{2,34},{34,2},{3,35},{35,3},{4,36},{36... | collective-permute-start | bytes 786440 | tf_op jit(solution)/shard_map/ppermute | solution.py:472
  2.8 0.1 collective-permute-start.3
  2.9 1.5 %collective-permute-start.6 = (f32[16,8,128]{2,1,0:T(8,128)S(1)}, f32[16,8,128]{2,1,0:T(8,128)S(1)}, u32[]{:S(2)}, u32[]{:S(2)}) collective-permute-start(f32[16,8,128]{2,1,0:T(8,128)S(1)} %get-tuple-element.40), channel_id=1, source_target_pairs={{0,96},{32,64},{64,32},{96,0},{1,97},{33,65},{65,33},{97,1},{2,98}... | collective-permute-start | bytes 196616 | tf_op jit(solution)/shard_map/ppermute | solution.py:471
  4.4 2.6 %collective-permute-done.6.zo.z = f32[16,8,128]{2,1,0:T(8,128)S(1)} collective-permute-done((f32[16,8,128]{2,1,0:T(8,128)S(1)}, f32[16,8,128]{2,1,0:T(8,128)S(1)}, u32[]{:S(2)}, u32[]{:S(2)}) %collective-permute-start.6) | collective-permute-done | bytes 65568 | tf_op jit(solution)/shard_map/ppermute | solution.py:471
  7.1 0.0 collective-permute-done.uo.u
  7.1 0.0 collective-permute-done.1.po.p
  7.1 0.0 collective-permute-done.2.lo.l
  7.1 0.0 collective-permute-done.3.so.s
  7.1 0.5 %shard_map.68 = f32[16,8,128]{2,1,0:T(8,128)S(1)} custom-call(f32[64,8,128]{2,1,0:T(8,128)S(1)} %collective-permute-done.uo.u, f32[64,8,128]{2,1,0:T(8,128)S(1)} %collective-permute-done.1.po.p, f32[64,8,128]{2,1,0:T(8,128)S(1)} %collective-permute-done.2.lo.l, f32[64,8,128]{2,1,0:T(8,128)S(1)} %collective-permute-done.3.so.s, ...), custom_call_target="tpu_custom_call" | custom-call | flops 1 | tf_op jit(solution)/shard_map/pallas_call | solution.py:424
  7.6 4.7 %collective-permute-start.8 = (f32[16,8,128]{2,1,0:T(8,128)S(1)}, f32[16,8,128]{2,1,0:T(8,128)S(1)}, u32[]{:S(2)}, u32[]{:S(2)}) collective-permute-start(f32[16,8,128]{2,1,0:T(8,128)S(1)} %shard_map.68), channel_id=1, source_target_pairs={{0,97},{97,0},{1,98},{98,1},{2,99},{99,2},{3,100},{100,3},{4,101},... | collective-permute-start | bytes 196616 | tf_op jit(solution)/shard_map/ppermute | solution.py:481
  12.3 1.4 %shard_map.65 = (f32[2,2,64,8,128]{4,3,2,1,0:T(8,128)S(1)}, f32[3,2,64,8,128]{4,3,2,1,0:T(8,128)S(1)}, f32[2,64,8,128]{3,2,1,0:T(8,128)S(1)}, f32[4,8,128]{2,1,0:T(8,128)S(1)}, f32[18,8,128]{2,1,0:T(8,128)S(1)}) custom-call(f32[64,8,128]{2,1,0:T(8,128)S(1)} %get-tuple-element.27.u, f32[64,8,128]{2,1,0:T(8,128)S(1)} %get-tuple-element.28.p, ...), custom_call_target="tpu_custom_call" | custom-call | flops 1 | tf_op jit(solution)/shard_map/pallas_call | solution.py:424
  13.7 2.3 %collective-permute-start.4 = (f32[18,8,128]{2,1,0:T(8,128)S(1)}, f32[18,8,128]{2,1,0:T(8,128)S(1)}, u32[]{:S(2)}, u32[]{:S(2)}) collective-permute-start(f32[18,8,128]{2,1,0:T(8,128)S(1)} %get-tuple-element.35), channel_id=1, source_target_pairs={{0,96},{32,64},{64,32},{96,0},{1,97},{33,65},{65,33},{97,1},{2,98}... | collective-permute-start | bytes 221192 | tf_op jit(solution)/shard_map/ppermute | solution.py:477
  16.0 0.4 %collective-permute-start.7 = (f32[16,8,128]{2,1,0:T(8,128)S(1)}, f32[16,8,128]{2,1,0:T(8,128)S(1)}, u32[]{:S(2)}, u32[]{:S(2)}) collective-permute-start(f32[16,8,128]{2,1,0:T(8,128)S(1)} %collective-permute-done.6.zo.z), channel_id=1, source_target_pairs={{0,32},{32,0},{1,33},{33,1},{2,34},{34,2},{3,35},{35,3},{4,36},{36... | collective-permute-start | bytes 196616 | tf_op jit(solution)/shard_map/ppermute | solution.py:479
  16.4 0.0 collective-permute-done.8.b
  16.4 0.1 collective-permute-start.9
  16.5 2.0 %collective-permute-done.4.far = f32[18,8,128]{2,1,0:T(8,128)S(1)} collective-permute-done((f32[18,8,128]{2,1,0:T(8,128)S(1)}, f32[18,8,128]{2,1,0:T(8,128)S(1)}, u32[]{:S(2)}, u32[]{:S(2)}) %collective-permute-start.4) | collective-permute-done | bytes 73760 | tf_op jit(solution)/shard_map/ppermute | solution.py:477
  18.5 1.7 %shard_map.66 = (f32[2,2,64,8,128]{4,3,2,1,0:T(8,128)S(1)}, f32[2,64,8,128]{3,2,1,0:T(8,128)S(1)}, f32[4,8,128]{2,1,0:T(8,128)S(1)}, f32[12,8,128]{2,1,0:T(8,128)S(1)}) custom-call(f32[4,8,128]{2,1,0:T(8,128)S(1)} %get-tuple-element.26.ish, f32[2,2,64,8,128]{4,3,2,1,0:T(8,128)S(1)} %get-tuple-element.31.g, f32[3,2,64,8,128]{4,3,2,1,0:T(8,128)S(1)} %get-tuple-element.32.c, ...), custom_call_target="tpu_custom_call" | custom-call | flops 1 | tf_op jit(solution)/shard_map/pallas_call | solution.py:424
  20.2 1.5 %collective-permute-start.5 = (f32[12,8,128]{2,1,0:T(8,128)S(1)}, f32[12,8,128]{2,1,0:T(8,128)S(1)}, u32[]{:S(2)}, u32[]{:S(2)}) collective-permute-start(f32[12,8,128]{2,1,0:T(8,128)S(1)} %get-tuple-element.39), channel_id=1, source_target_pairs={{0,96},{32,64},{64,32},{96,0},{1,97},{33,65},{65,33},{97,1},{2,98}... | collective-permute-start | bytes 147464 | tf_op jit(solution)/shard_map/ppermute | solution.py:489
  21.8 0.0 collective-permute-done.7.z
  21.8 0.9 %shard_map.67.v_ref = f32[4,64,8,128]{3,2,1,0:T(8,128)S(1)} custom-call(f32[64,8,128]{2,1,0:T(8,128)S(1)} %get-tuple-element.27.u, f32[64,8,128]{2,1,0:T(8,128)S(1)} %get-tuple-element.28.p, f32[64,8,128]{2,1,0:T(8,128)S(1)} %get-tuple-element.29.l, f32[64,8,128]{2,1,0:T(8,128)S(1)} %get-tuple-element.30.s, f32[64,8,128]{2,1,0:T(8,128)S(1)} %collective-permute-done.uo.u, ...), custom_call_target="tpu_custom_call" | custom-call | flops 1 | tf_op jit(solution)/shard_map/pallas_call | solution.py:424
  22.7 0.0 collective-permute-done.9.bo
  22.7 0.7 %shard_map.69 = (f32[4,64,8,128]{3,2,1,0:T(8,128)S(1)}, f32[3,64,8,128]{3,2,1,0:T(8,128)S(1)}, f32[64,8,128]{2,1,0:T(8,128)S(1)}, f32[4,8,128]{2,1,0:T(8,128)S(1)}) custom-call(f32[4,64,8,128]{3,2,1,0:T(8,128)S(1)} %shard_map.67.v_ref, f32[16,8,128]{2,1,0:T(8,128)S(1)} %collective-permute-done.8.b, f32[16,8,128]{2,1,0:T(8,128)S(1)} %collective-permute-done.9.bo, ...), custom_call_target="tpu_custom_call" | custom-call | flops 1 | tf_op jit(solution)/shard_map/pallas_call | solution.py:424
  23.4 1.6 %shard_map.70 = (f32[64,8,128]{2,1,0:T(8,128)S(1)}, f32[2,8,128]{2,1,0:T(8,128)S(1)}) custom-call(f32[4,64,8,128]{3,2,1,0:T(8,128)S(1)} %get-tuple-element.41.g_ref, f32[3,64,8,128]{3,2,1,0:T(8,128)S(1)} %get-tuple-element.42.c_ref, f32[64,8,128]{2,1,0:T(8,128)S(1)} %get-tuple-element.43.d_in, f32[4,8,128]{2,1,0:T(8,128)S(1)} %get-tuple-element.44.rest_ref, ...), custom_call_target="tpu_custom_call" | custom-call | flops 1 | tf_op jit(solution)/shard_map/pallas_call | solution.py:424
  25.0 0.4 %collective-permute-start.10 = (f32[2,8,128]{2,1,0:T(8,128)S(1)}, f32[2,8,128]{2,1,0:T(8,128)S(1)}, u32[]{:S(2)}, u32[]{:S(2)}) collective-permute-start(f32[2,8,128]{2,1,0:T(8,128)S(1)} %get-tuple-element.46), channel_id=1, source_target_pairs={{0,96},{32,64},{64,32},{96,0},{1,97},{33,65},{65,33},{97,1},{2,98}... | collective-permute-start | bytes 24584 | tf_op jit(solution)/shard_map/ppermute | solution.py:497
  25.4 0.0 collective-permute-done.5.far
  25.4 0.5 %shard_map.71.value = f32[64,8,128]{2,1,0:T(8,128)S(1)} custom-call(f32[4,8,128]{2,1,0:T(8,128)S(1)} %get-tuple-element.26.ish, f32[2,2,64,8,128]{4,3,2,1,0:T(8,128)S(1)} %get-tuple-element.36.g, f32[3,2,64,8,128]{4,3,2,1,0:T(8,128)S(1)} %get-tuple-element.32.c, f32[2,64,8,128]{3,2,1,0:T(8,128)S(1)} %get-tuple-element.37.d, ...), custom_call_target="tpu_custom_call" | custom-call | flops 1 | tf_op jit(solution)/shard_map/pallas_call | solution.py:424
  25.9 2.3 %collective-permute-done.10.far = f32[2,8,128]{2,1,0:T(8,128)S(1)} collective-permute-done((f32[2,8,128]{2,1,0:T(8,128)S(1)}, f32[2,8,128]{2,1,0:T(8,128)S(1)}, u32[]{:S(2)}, u32[]{:S(2)}) %collective-permute-start.10) | collective-permute-done | bytes 8224 | tf_op jit(solution)/shard_map/ppermute | solution.py:497
  28.2 0.8 %shard_map.72 = f32[64,8,128]{2,1,0:T(8,128)} custom-call(f32[64,8,128]{2,1,0:T(8,128)S(1)} %shard_map.71.value, f32[2,8,128]{2,1,0:T(8,128)S(1)} %collective-permute-done.10.far), custom_call_target="tpu_custom_call" | custom-call | flops 1 | tf_op jit(solution)/shard_map/pallas_call | solution.py:424
Async XLA Ops:
  1.6 5.5 %collective-permute-start = (f32[64,8,128]{2,1,0:T(8,128)S(1)}, f32[64,8,128]{2,1,0:T(8,128)S(1)}, u32[]{:S(2)}, u32[]{:S(2)}) collective-permute-start(f32[64,8,128]{2,1,0:T(8,128)S(1)} %get-tuple-element.27.u), channel_id=1, source_target_pairs={{0,32},{32,0},{1,33},{33,1},{2,34},{34,2},{3,35},{35,3},{4,36},{36... | collective-permute-start | bytes 786440 | tf_op jit(solution)/shard_map/ppermute | solution.py:472
  2.3 4.8 %collective-permute-start.1 = (f32[64,8,128]{2,1,0:T(8,128)S(1)}, f32[64,8,128]{2,1,0:T(8,128)S(1)}, u32[]{:S(2)}, u32[]{:S(2)}) collective-permute-start(f32[64,8,128]{2,1,0:T(8,128)S(1)} %get-tuple-element.28.p), channel_id=1, source_target_pairs={{0,32},{32,0},{1,33},{33,1},{2,34},{34,2},{3,35},{35,3},{4,36},{36... | collective-permute-start | bytes 786440 | tf_op jit(solution)/shard_map/ppermute | solution.py:472
  2.4 4.7 %collective-permute-start.2 = (f32[64,8,128]{2,1,0:T(8,128)S(1)}, f32[64,8,128]{2,1,0:T(8,128)S(1)}, u32[]{:S(2)}, u32[]{:S(2)}) collective-permute-start(f32[64,8,128]{2,1,0:T(8,128)S(1)} %get-tuple-element.29.l), channel_id=1, source_target_pairs={{0,32},{32,0},{1,33},{33,1},{2,34},{34,2},{3,35},{35,3},{4,36},{36... | collective-permute-start | bytes 786440 | tf_op jit(solution)/shard_map/ppermute | solution.py:472
  2.8 4.3 %collective-permute-start.3 = (f32[64,8,128]{2,1,0:T(8,128)S(1)}, f32[64,8,128]{2,1,0:T(8,128)S(1)}, u32[]{:S(2)}, u32[]{:S(2)}) collective-permute-start(f32[64,8,128]{2,1,0:T(8,128)S(1)} %get-tuple-element.30.s), channel_id=1, source_target_pairs={{0,32},{32,0},{1,33},{33,1},{2,34},{34,2},{3,35},{35,3},{4,36},{36... | collective-permute-start | bytes 786440 | tf_op jit(solution)/shard_map/ppermute | solution.py:472
  2.9 4.1 %collective-permute-start.6 = (f32[16,8,128]{2,1,0:T(8,128)S(1)}, f32[16,8,128]{2,1,0:T(8,128)S(1)}, u32[]{:S(2)}, u32[]{:S(2)}) collective-permute-start(f32[16,8,128]{2,1,0:T(8,128)S(1)} %get-tuple-element.40), channel_id=1, source_target_pairs={{0,96},{32,64},{64,32},{96,0},{1,97},{33,65},{65,33},{97,1},{2,98}... | collective-permute-start | bytes 196616 | tf_op jit(solution)/shard_map/ppermute | solution.py:471
  7.6 8.8 %collective-permute-start.8 = (f32[16,8,128]{2,1,0:T(8,128)S(1)}, f32[16,8,128]{2,1,0:T(8,128)S(1)}, u32[]{:S(2)}, u32[]{:S(2)}) collective-permute-start(f32[16,8,128]{2,1,0:T(8,128)S(1)} %shard_map.68), channel_id=1, source_target_pairs={{0,97},{97,0},{1,98},{98,1},{2,99},{99,2},{3,100},{100,3},{4,101},... | collective-permute-start | bytes 196616 | tf_op jit(solution)/shard_map/ppermute | solution.py:481
  13.7 4.9 %collective-permute-start.4 = (f32[18,8,128]{2,1,0:T(8,128)S(1)}, f32[18,8,128]{2,1,0:T(8,128)S(1)}, u32[]{:S(2)}, u32[]{:S(2)}) collective-permute-start(f32[18,8,128]{2,1,0:T(8,128)S(1)} %get-tuple-element.35), channel_id=1, source_target_pairs={{0,96},{32,64},{64,32},{96,0},{1,97},{33,65},{65,33},{97,1},{2,98}... | collective-permute-start | bytes 221192 | tf_op jit(solution)/shard_map/ppermute | solution.py:477
  16.0 5.8 %collective-permute-start.7 = (f32[16,8,128]{2,1,0:T(8,128)S(1)}, f32[16,8,128]{2,1,0:T(8,128)S(1)}, u32[]{:S(2)}, u32[]{:S(2)}) collective-permute-start(f32[16,8,128]{2,1,0:T(8,128)S(1)} %collective-permute-done.6.zo.z), channel_id=1, source_target_pairs={{0,32},{32,0},{1,33},{33,1},{2,34},{34,2},{3,35},{35,3},{4,36},{36... | collective-permute-start | bytes 196616 | tf_op jit(solution)/shard_map/ppermute | solution.py:479
  16.4 6.3 %collective-permute-start.9 = (f32[16,8,128]{2,1,0:T(8,128)S(1)}, f32[16,8,128]{2,1,0:T(8,128)S(1)}, u32[]{:S(2)}, u32[]{:S(2)}) collective-permute-start(f32[16,8,128]{2,1,0:T(8,128)S(1)} %collective-permute-done.8.b), channel_id=1, source_target_pairs={{0,32},{32,0},{1,33},{33,1},{2,34},{34,2},{3,35},{35,3},{4,36},{36... | collective-permute-start | bytes 196616 | tf_op jit(solution)/shard_map/ppermute | solution.py:482
  20.2 5.2 %collective-permute-start.5 = (f32[12,8,128]{2,1,0:T(8,128)S(1)}, f32[12,8,128]{2,1,0:T(8,128)S(1)}, u32[]{:S(2)}, u32[]{:S(2)}) collective-permute-start(f32[12,8,128]{2,1,0:T(8,128)S(1)} %get-tuple-element.39), channel_id=1, source_target_pairs={{0,96},{32,64},{64,32},{96,0},{1,97},{33,65},{65,33},{97,1},{2,98}... | collective-permute-start | bytes 147464 | tf_op jit(solution)/shard_map/ppermute | solution.py:489
  25.0 3.2 %collective-permute-start.10 = (f32[2,8,128]{2,1,0:T(8,128)S(1)}, f32[2,8,128]{2,1,0:T(8,128)S(1)}, u32[]{:S(2)}, u32[]{:S(2)}) collective-permute-start(f32[2,8,128]{2,1,0:T(8,128)S(1)} %get-tuple-element.46), channel_id=1, source_target_pairs={{0,96},{32,64},{64,32},{96,0},{1,97},{33,65},{65,33},{97,1},{2,98}... | collective-permute-start | bytes 24584 | tf_op jit(solution)/shard_map/ppermute | solution.py:497

commit v3 on v2

--- a/solution.py
+++ b/solution.py
@@ -89,13 +89,15 @@
     return own * (inverse * shift - 4.0 * a1) + (a1 * around + a2)
 
 
-def explicit(rows, up, c, m, shift, f_ref, which=(0, 1)):
-    sums = rows.around(*up)
-    for x in which:
-        f_ref[x, m] = forcing(up[x], sums[x], c[0, x, m], c[1, x, m], c[2, x, m], shift)
-
-
-def reach(h, rows, shift, g, c, d, which):
+def explicit(rows, u_ref, c, shift, f_ref, which=(0, 1)):
+    for m in range(L):
+        up = [u_ref[x, m] for x in range(2)]
+        sums = rows.around(*up)
+        for x in which:
+            f_ref[x, m] = forcing(up[x], sums[x], c[0, x, m], c[1, x, m], c[2, x, m], shift)
+
+
+def reach(h, rows, shift, g, c, d, which, u_ref, t_ref):
     one = jnp.full((ROWS, COLS), 1.0, F32)
     zero = jnp.zeros((ROWS, COLS), F32)
     up, to, on = [zero] * 2, [one] * 2, [one] * 2
@@ -104,6 +106,11 @@
         for x in range(2):
             up[x] = d[x, m] + g[h, x, m] * up[x]
             to[x] = to[x] * g[h, x, m]
+            u_ref[x, m] = up[x]
+            t_ref[x, m] = to[x]
+    for m in range(L - 1, -1, -1):
+        up = [u_ref[x, m] for x in range(2)]
+        to = [t_ref[x, m] for x in range(2)]
         around = rows.around(*up)
         beside = rows.beside(*to)
         for x in which:
@@ -175,7 +182,9 @@
         out[q] = acc
 
 
-def first_kernel(u, p, l, s, uo, po, lo, so, ish, g_out, c_out, d_out, rest_out, pay):
+def first_kernel(
+    u, p, l, s, uo, po, lo, so, ish, g_out, c_out, d_out, rest_out, pay, f_ref, t_ref
+):
     rows = Rows()
     shift = [ish[h] for h in range(2)]
     one = jnp.full((ROWS, COLS), 1.0, F32)
@@ -192,14 +201,16 @@
             c_out[0, x, m] = inverse
             c_out[1, x, m] = a1
             c_out[2, x, m] = a2
-            f = forcing(fields[x], sums[x], inverse, a1, a2, shift[0])
+            f_ref[x, m] = forcing(fields[x], sums[x], inverse, a1, a2, shift[0])
+    for m in range(L):
+        for x in range(2):
             for h in range(2):
-                g, rest[h][x] = factor(inverse, shift[h], rest[h][x])
+                g, rest[h][x] = factor(c_out[0, x, m], shift[h], rest[h][x])
                 g_out[h, x, m] = g
                 if h == 0:
-                    d[x] = g * (d[x] + f)
+                    d[x] = g * (d[x] + f_ref[x, m])
                     d_out[x, m] = d[x]
-    total = reach(0, rows, shift[1], g_out, c_out, d_out, (0, 1))
+    total = reach(0, rows, shift[1], g_out, c_out, d_out, (0, 1), f_ref, t_ref)
     for x in range(2):
         pay[x] = d[x]
         for h in range(2):
@@ -210,7 +221,7 @@
             pay[6 + 6 * x + i] = total[x][i]
 
 
-def middle_kernel(ish, g, c, d, rest, far, g_out, d_out, rest_out, pay, f_ref, d_ref):
+def middle_kernel(ish, g, c, d, rest, far, g_out, d_out, rest_out, pay, f_ref, d_ref, t_ref):
     rows = Rows()
     zero = jnp.zeros((ROWS, COLS), F32)
 
@@ -220,9 +231,11 @@
     up = [meet(d[x, L - 1], rest[x], far[1 - x], far_rest(0, x)) for x in range(2)]
     for m in range(L - 1, -1, -1):
         up = [d[x, m] + g[0, x, m] * up[x] for x in range(2)]
+        for x in range(2):
+            t_ref[x, m] = up[x]
         if m == L - 1:
             last = up
-        explicit(rows, up, c, m, ish[1], f_ref)
+    explicit(rows, t_ref, c, ish[1], f_ref)
     one = jnp.full((ROWS, COLS), 1.0, F32)
     after = [[(one, one)] * 2 for _ in range(2)]
     now = [zero, zero]
@@ -236,13 +249,15 @@
     up = [meet(now[x], rest[2 + x], far_d[x], far_rest(1, x)) for x in range(2)]
     for m in range(L - 1, -1, -1):
         up = [d_ref[x, m] + g[1, x, m] * up[x] for x in range(2)]
-        explicit(rows, up, c, m, ish[2], f_ref)
+        for x in range(2):
+            t_ref[x, m] = up[x]
+    explicit(rows, t_ref, c, ish[2], f_ref)
     now = [zero, zero]
     for m in range(L):
         for x in range(2):
             now[x] = g_out[0, x, m] * (now[x] + f_ref[x, m])
             d_out[x, m] = now[x]
-    total = reach(0, rows, ish[3], g_out, c, d_out, (1,))
+    total = reach(0, rows, ish[3], g_out, c, d_out, (1,), f_ref, t_ref)
     for x in range(2):
         pay[x] = now[x]
         for h in range(2):
@@ -259,16 +274,18 @@
     return (lane >= zone) & (lane < zone + 4)
 
 
-def finish_kernel(ish, g, c, d, rest, far, edge, out, f_ref, d_ref):
+def finish_kernel(ish, g, c, d, rest, far, edge, out, f_ref, d_ref, t_ref):
     rows = Rows()
     side = zone_side()
     here = own_columns(side)
     up = [meet(d[x, L - 1], rest[x], far[1 - x], far[8 + 1 - x]) for x in range(2)]
     for m in range(L - 1, -1, -1):
         up = [d[x, m] + g[0, x, m] * up[x] for x in range(2)]
+        for x in range(2):
+            t_ref[x, m] = up[x]
         if m == L - 1:
             last = up
-        explicit(rows, up, c, m, ish[3], f_ref, (0,))
+    explicit(rows, t_ref, c, ish[3], f_ref, (0,))
     now = jnp.zeros((ROWS, COLS), F32)
     for m in range(L):
         now = g[1, 0, m] * (now + f_ref[0, m])
@@ -385,11 +402,15 @@
     lane = lanes()
     side = zone_side()
     zero = jnp.zeros((ROWS, COLS), F32)
+    joints = []
+    for h in range(HALF):
+        rest, far_rest = rest_ref[h], groups.far(rest_ref[h])
+        joints.append((1.0 - far_rest, 1.0 / (rest + far_rest - rest * far_rest)))
     d = d_in[L - 1]
     for h in range(HALF):
         source = d_in if h == 0 else d_ref
-        rest = rest_ref[h]
-        up = meet(d, rest, groups.far(d), groups.far(rest))
+        far_g, inverse_joint = joints[h]
+        up = (groups.far(d) + far_g * d) * inverse_joint
         if h == HALF - 1:
             acc = zero
             for m in range(L - 1, -1, -1):
@@ -472,7 +493,8 @@
     oth = [lax.ppermute(a, "gx", SWAP) for a in own]
 
     g, c, d, rest, pay = call(
-        first_kernel, (shape(2, 2, L), shape(3, 2, L), shape(2, L), shape(4), shape(18))
+        first_kernel, (shape(2, 2, L), shape(3, 2, L), shape(2, L), shape(4), shape(18)),
+        (shape(2, L), shape(2, L)),
     )(*own, *oth, ish)
     far = lax.ppermute(pay, ZX, CROSS)
 
@@ -484,7 +506,7 @@
     g, d, rest, pay = call(
         middle_kernel,
         (shape(2, 2, L), shape(2, L), shape(4), shape(12)),
-        (shape(2, L), shape(2, L)),
+        (shape(2, L), shape(2, L), shape(2, L)),
     )(ish, g, c, d, rest, far)
     far = lax.ppermute(pay, ZX, CROSS)
     local = call(edge_local_kernel, shape(4, L), (whole,))(*own, *oth, z_in, z_oth)
@@ -495,7 +517,9 @@
     )(local, in_b, b_oth, ish)
     edge, back = call(edge_rest_kernel, (whole, shape(2)), (whole, whole))(eg, ec, ed, er, ish)
     back = lax.ppermute(back, ZX, CROSS)
-    value = call(finish_kernel, whole, (shape(1, L), whole))(ish, g, c, d, rest, far, edge)
+    value = call(finish_kernel, whole, (shape(1, L), whole, shape(2, L)))(
+        ish, g, c, d, rest, far, edge
+    )
     return call(
         last_kernel, whole, (whole, pltpu.SemaphoreType.DMA((L // CHUNK,))), out_spec=HBM
     )(value, back)

time: 29.2 us -> 29.1 us (level)
  transfers between devices with their start and end apart: 11 -> 11, of which waited for: 3 -> 3; matrix products, arithmetic and copies ran while one was open for 0% -> 0% of each run, Pallas kernels for 24% -> 23%
where the time goes in v3:
time: 29.1 us; the launch traced here: 28.9 us
  starting transfers between devices  12.3 us (42%)
  Pallas kernels  9.62 us (33%)
  waiting for transfers between devices  6.93 us (24%)
    pallas_call x9, Pallas kernels, run(): pl.pallas_call(body, out_shape=outs, in_specs=[specs] * len(args), out_sp...  9.62 us
    ppermute x1, starting transfers between devices, on_device(): in_b = lax.ppermute(out_b, ('gz', 'gx', 'gy'), side_pairs(size))  4.67 us
    ppermute x2, starting transfers between devices, on_device(): far = lax.ppermute(pay, ZX, CROSS)  3.87 us
    ppermute x1, waiting for transfers between devices, on_device(): z_oth = lax.ppermute(z_out, ZX, CROSS)  2.63 us
    ppermute x1, waiting for transfers between devices, on_device(): back = lax.ppermute(back, ZX, CROSS)  2.27 us
    ppermute x2, waiting for transfers between devices, on_device(): far = lax.ppermute(pay, ZX, CROSS)  2.02 us
    ppermute x1, starting transfers between devices, on_device(): z_oth = lax.ppermute(z_out, ZX, CROSS)  1.51 us
    ppermute x4, starting transfers between devices, on_device(): oth = [lax.ppermute(a, 'gx', SWAP) for a in own]  1.36 us
  transfers between devices with their start and end apart: 11, of which 3 were waited for; matrix products, arithmetic and copies ran while one was open for 0% of the time, Pallas kernels for 23%

profile of v3, /device:TPU:97, one launch (start us, length us, event | category | flops | bytes accessed | tf_op | source)
XLA Modules:
  0.0 28.9 jit_solution(108737478679247674)
XLA Ops:
  0.0 1.6 %shard_map.64 = (f32[64,8,128]{2,1,0:T(8,128)S(1)}, f32[64,8,128]{2,1,0:T(8,128)S(1)}, f32[64,8,128]{2,1,0:T(8,128)S(1)}, f32[64,8,128]{2,1,0:T(8,128)S(1)}, f32...) custom-call(f32[64,8,128]{2,1,0:T(8,128)} %u_in.1, f32[64,8,128]{2,1,0:T(8,128)} %p_in.1, f32[64,8,128]{2,1,0:T(8,128)} %l_in.1, ...), custom_call_target="tpu_custom_call" | custom-call | flops 1 | tf_op jit(solution)/shard_map/pallas_call | solution.py:445
  1.6 0.8 %collective-permute-start = (f32[64,8,128]{2,1,0:T(8,128)S(1)}, f32[64,8,128]{2,1,0:T(8,128)S(1)}, u32[]{:S(2)}, u32[]{:S(2)}) collective-permute-start(f32[64,8,128]{2,1,0:T(8,128)S(1)} %get-tuple-element.27.u), channel_id=1, source_target_pairs={{0,32},{32,0},{1,33},{33,1},{2,34},{34,2},{3,35},{35,3},{4,36},{36... | collective-permute-start | bytes 786440 | tf_op jit(solution)/shard_map/ppermute | solution.py:493
  2.3 0.1 collective-permute-start.1
  2.4 0.4 %collective-permute-start.2 = (f32[64,8,128]{2,1,0:T(8,128)S(1)}, f32[64,8,128]{2,1,0:T(8,128)S(1)}, u32[]{:S(2)}, u32[]{:S(2)}) collective-permute-start(f32[64,8,128]{2,1,0:T(8,128)S(1)} %get-tuple-element.29.l), channel_id=1, source_target_pairs={{0,32},{32,0},{1,33},{33,1},{2,34},{34,2},{3,35},{35,3},{4,36},{36... | collective-permute-start | bytes 786440 | tf_op jit(solution)/shard_map/ppermute | solution.py:493
  2.8 0.1 collective-permute-start.3
  2.9 1.5 %collective-permute-start.6 = (f32[16,8,128]{2,1,0:T(8,128)S(1)}, f32[16,8,128]{2,1,0:T(8,128)S(1)}, u32[]{:S(2)}, u32[]{:S(2)}) collective-permute-start(f32[16,8,128]{2,1,0:T(8,128)S(1)} %get-tuple-element.40), channel_id=1, source_target_pairs={{0,96},{32,64},{64,32},{96,0},{1,97},{33,65},{65,33},{97,1},{2,98}... | collective-permute-start | bytes 196616 | tf_op jit(solution)/shard_map/ppermute | solution.py:492
  4.4 2.6 %collective-permute-done.6.zo.z = f32[16,8,128]{2,1,0:T(8,128)S(1)} collective-permute-done((f32[16,8,128]{2,1,0:T(8,128)S(1)}, f32[16,8,128]{2,1,0:T(8,128)S(1)}, u32[]{:S(2)}, u32[]{:S(2)}) %collective-permute-start.6) | collective-permute-done | bytes 65568 | tf_op jit(solution)/shard_map/ppermute | solution.py:492
  7.1 0.0 collective-permute-done.uo.u
  7.1 0.0 collective-permute-done.1.po.p
  7.1 0.0 collective-permute-done.2.lo.l
  7.1 0.0 collective-permute-done.3.so.s
  7.1 0.5 %shard_map.68 = f32[16,8,128]{2,1,0:T(8,128)S(1)} custom-call(f32[64,8,128]{2,1,0:T(8,128)S(1)} %collective-permute-done.uo.u, f32[64,8,128]{2,1,0:T(8,128)S(1)} %collective-permute-done.1.po.p, f32[64,8,128]{2,1,0:T(8,128)S(1)} %collective-permute-done.2.lo.l, f32[64,8,128]{2,1,0:T(8,128)S(1)} %collective-permute-done.3.so.s, ...), custom_call_target="tpu_custom_call" | custom-call | flops 1 | tf_op jit(solution)/shard_map/pallas_call | solution.py:445
  7.6 4.7 %collective-permute-start.8 = (f32[16,8,128]{2,1,0:T(8,128)S(1)}, f32[16,8,128]{2,1,0:T(8,128)S(1)}, u32[]{:S(2)}, u32[]{:S(2)}) collective-permute-start(f32[16,8,128]{2,1,0:T(8,128)S(1)} %shard_map.68), channel_id=1, source_target_pairs={{0,97},{97,0},{1,98},{98,1},{2,99},{99,2},{3,100},{100,3},{4,101},... | collective-permute-start | bytes 196616 | tf_op jit(solution)/shard_map/ppermute | solution.py:503
  12.3 1.4 %shard_map.65 = (f32[2,2,64,8,128]{4,3,2,1,0:T(8,128)S(1)}, f32[3,2,64,8,128]{4,3,2,1,0:T(8,128)S(1)}, f32[2,64,8,128]{3,2,1,0:T(8,128)S(1)}, f32[4,8,128]{2,1,0:T(8,128)S(1)}, f32[18,8,128]{2,1,0:T(8,128)S(1)}) custom-call(f32[64,8,128]{2,1,0:T(8,128)S(1)} %get-tuple-element.27.u, f32[64,8,128]{2,1,0:T(8,128)S(1)} %get-tuple-element.28.p, ...), custom_call_target="tpu_custom_call" | custom-call | flops 1 | tf_op jit(solution)/shard_map/pallas_call | solution.py:445
  13.6 2.3 %collective-permute-start.4 = (f32[18,8,128]{2,1,0:T(8,128)S(1)}, f32[18,8,128]{2,1,0:T(8,128)S(1)}, u32[]{:S(2)}, u32[]{:S(2)}) collective-permute-start(f32[18,8,128]{2,1,0:T(8,128)S(1)} %get-tuple-element.35), channel_id=1, source_target_pairs={{0,96},{32,64},{64,32},{96,0},{1,97},{33,65},{65,33},{97,1},{2,98}... | collective-permute-start | bytes 221192 | tf_op jit(solution)/shard_map/ppermute | solution.py:499
  16.0 0.4 %collective-permute-start.7 = (f32[16,8,128]{2,1,0:T(8,128)S(1)}, f32[16,8,128]{2,1,0:T(8,128)S(1)}, u32[]{:S(2)}, u32[]{:S(2)}) collective-permute-start(f32[16,8,128]{2,1,0:T(8,128)S(1)} %collective-permute-done.6.zo.z), channel_id=1, source_target_pairs={{0,32},{32,0},{1,33},{33,1},{2,34},{34,2},{3,35},{35,3},{4,36},{36... | collective-permute-start | bytes 196616 | tf_op jit(solution)/shard_map/ppermute | solution.py:501
  16.4 0.0 collective-permute-done.8.b
  16.4 0.1 collective-permute-start.9
  16.5 2.0 %collective-permute-done.4.far = f32[18,8,128]{2,1,0:T(8,128)S(1)} collective-permute-done((f32[18,8,128]{2,1,0:T(8,128)S(1)}, f32[18,8,128]{2,1,0:T(8,128)S(1)}, u32[]{:S(2)}, u32[]{:S(2)}) %collective-permute-start.4) | collective-permute-done | bytes 73760 | tf_op jit(solution)/shard_map/ppermute | solution.py:499
  18.5 1.6 %shard_map.66 = (f32[2,2,64,8,128]{4,3,2,1,0:T(8,128)S(1)}, f32[2,64,8,128]{3,2,1,0:T(8,128)S(1)}, f32[4,8,128]{2,1,0:T(8,128)S(1)}, f32[12,8,128]{2,1,0:T(8,128)S(1)}) custom-call(f32[4,8,128]{2,1,0:T(8,128)S(1)} %get-tuple-element.26.ish, f32[2,2,64,8,128]{4,3,2,1,0:T(8,128)S(1)} %get-tuple-element.31.g, f32[3,2,64,8,128]{4,3,2,1,0:T(8,128)S(1)} %get-tuple-element.32.c, ...), custom_call_target="tpu_custom_call" | custom-call | flops 1 | tf_op jit(solution)/shard_map/pallas_call | solution.py:445
  20.1 1.5 %collective-permute-start.5 = (f32[12,8,128]{2,1,0:T(8,128)S(1)}, f32[12,8,128]{2,1,0:T(8,128)S(1)}, u32[]{:S(2)}, u32[]{:S(2)}) collective-permute-start(f32[12,8,128]{2,1,0:T(8,128)S(1)} %get-tuple-element.39), channel_id=1, source_target_pairs={{0,96},{32,64},{64,32},{96,0},{1,97},{33,65},{65,33},{97,1},{2,98}... | collective-permute-start | bytes 147464 | tf_op jit(solution)/shard_map/ppermute | solution.py:511
  21.7 0.0 collective-permute-done.7.z
  21.7 0.9 %shard_map.67.v_ref = f32[4,64,8,128]{3,2,1,0:T(8,128)S(1)} custom-call(f32[64,8,128]{2,1,0:T(8,128)S(1)} %get-tuple-element.27.u, f32[64,8,128]{2,1,0:T(8,128)S(1)} %get-tuple-element.28.p, f32[64,8,128]{2,1,0:T(8,128)S(1)} %get-tuple-element.29.l, f32[64,8,128]{2,1,0:T(8,128)S(1)} %get-tuple-element.30.s, f32[64,8,128]{2,1,0:T(8,128)S(1)} %collective-permute-done.uo.u, ...), custom_call_target="tpu_custom_call" | custom-call | flops 1 | tf_op jit(solution)/shard_map/pallas_call | solution.py:445
  22.6 0.0 collective-permute-done.9.bo
  22.6 0.7 %shard_map.69 = (f32[4,64,8,128]{3,2,1,0:T(8,128)S(1)}, f32[3,64,8,128]{3,2,1,0:T(8,128)S(1)}, f32[64,8,128]{2,1,0:T(8,128)S(1)}, f32[4,8,128]{2,1,0:T(8,128)S(1)}) custom-call(f32[4,64,8,128]{3,2,1,0:T(8,128)S(1)} %shard_map.67.v_ref, f32[16,8,128]{2,1,0:T(8,128)S(1)} %collective-permute-done.8.b, f32[16,8,128]{2,1,0:T(8,128)S(1)} %collective-permute-done.9.bo, ...), custom_call_target="tpu_custom_call" | custom-call | flops 1 | tf_op jit(solution)/shard_map/pallas_call | solution.py:445
  23.3 1.6 %shard_map.70 = (f32[64,8,128]{2,1,0:T(8,128)S(1)}, f32[2,8,128]{2,1,0:T(8,128)S(1)}) custom-call(f32[4,64,8,128]{3,2,1,0:T(8,128)S(1)} %get-tuple-element.41.g_ref, f32[3,64,8,128]{3,2,1,0:T(8,128)S(1)} %get-tuple-element.42.c_ref, f32[64,8,128]{2,1,0:T(8,128)S(1)} %get-tuple-element.43.d_in, f32[4,8,128]{2,1,0:T(8,128)S(1)} %get-tuple-element.44.rest_ref, ...), custom_call_target="tpu_custom_call" | custom-call | flops 1 | tf_op jit(solution)/shard_map/pallas_call | solution.py:445
  24.9 0.4 %collective-permute-start.10 = (f32[2,8,128]{2,1,0:T(8,128)S(1)}, f32[2,8,128]{2,1,0:T(8,128)S(1)}, u32[]{:S(2)}, u32[]{:S(2)}) collective-permute-start(f32[2,8,128]{2,1,0:T(8,128)S(1)} %get-tuple-element.46), channel_id=1, source_target_pairs={{0,96},{32,64},{64,32},{96,0},{1,97},{33,65},{65,33},{97,1},{2,98}... | collective-permute-start | bytes 24584 | tf_op jit(solution)/shard_map/ppermute | solution.py:519
  25.3 0.0 collective-permute-done.5.far
  25.3 0.5 %shard_map.71.value = f32[64,8,128]{2,1,0:T(8,128)S(1)} custom-call(f32[4,8,128]{2,1,0:T(8,128)S(1)} %get-tuple-element.26.ish, f32[2,2,64,8,128]{4,3,2,1,0:T(8,128)S(1)} %get-tuple-element.36.g, f32[3,2,64,8,128]{4,3,2,1,0:T(8,128)S(1)} %get-tuple-element.32.c, f32[2,64,8,128]{3,2,1,0:T(8,128)S(1)} %get-tuple-element.37.d, ...), custom_call_target="tpu_custom_call" | custom-call | flops 1 | tf_op jit(solution)/shard_map/pallas_call | solution.py:445
  25.8 2.3 %collective-permute-done.10.far = f32[2,8,128]{2,1,0:T(8,128)S(1)} collective-permute-done((f32[2,8,128]{2,1,0:T(8,128)S(1)}, f32[2,8,128]{2,1,0:T(8,128)S(1)}, u32[]{:S(2)}, u32[]{:S(2)}) %collective-permute-start.10) | collective-permute-done | bytes 8224 | tf_op jit(solution)/shard_map/ppermute | solution.py:519
  28.1 0.8 %shard_map.72 = f32[64,8,128]{2,1,0:T(8,128)} custom-call(f32[64,8,128]{2,1,0:T(8,128)S(1)} %shard_map.71.value, f32[2,8,128]{2,1,0:T(8,128)S(1)} %collective-permute-done.10.far), custom_call_target="tpu_custom_call" | custom-call | flops 1 | tf_op jit(solution)/shard_map/pallas_call | solution.py:445
Async XLA Ops:
  1.6 5.5 %collective-permute-start = (f32[64,8,128]{2,1,0:T(8,128)S(1)}, f32[64,8,128]{2,1,0:T(8,128)S(1)}, u32[]{:S(2)}, u32[]{:S(2)}) collective-permute-start(f32[64,8,128]{2,1,0:T(8,128)S(1)} %get-tuple-element.27.u), channel_id=1, source_target_pairs={{0,32},{32,0},{1,33},{33,1},{2,34},{34,2},{3,35},{35,3},{4,36},{36... | collective-permute-start | bytes 786440 | tf_op jit(solution)/shard_map/ppermute | solution.py:493
  2.3 4.8 %collective-permute-start.1 = (f32[64,8,128]{2,1,0:T(8,128)S(1)}, f32[64,8,128]{2,1,0:T(8,128)S(1)}, u32[]{:S(2)}, u32[]{:S(2)}) collective-permute-start(f32[64,8,128]{2,1,0:T(8,128)S(1)} %get-tuple-element.28.p), channel_id=1, source_target_pairs={{0,32},{32,0},{1,33},{33,1},{2,34},{34,2},{3,35},{35,3},{4,36},{36... | collective-permute-start | bytes 786440 | tf_op jit(solution)/shard_map/ppermute | solution.py:493
  2.4 4.7 %collective-permute-start.2 = (f32[64,8,128]{2,1,0:T(8,128)S(1)}, f32[64,8,128]{2,1,0:T(8,128)S(1)}, u32[]{:S(2)}, u32[]{:S(2)}) collective-permute-start(f32[64,8,128]{2,1,0:T(8,128)S(1)} %get-tuple-element.29.l), channel_id=1, source_target_pairs={{0,32},{32,0},{1,33},{33,1},{2,34},{34,2},{3,35},{35,3},{4,36},{36... | collective-permute-start | bytes 786440 | tf_op jit(solution)/shard_map/ppermute | solution.py:493
  2.8 4.3 %collective-permute-start.3 = (f32[64,8,128]{2,1,0:T(8,128)S(1)}, f32[64,8,128]{2,1,0:T(8,128)S(1)}, u32[]{:S(2)}, u32[]{:S(2)}) collective-permute-start(f32[64,8,128]{2,1,0:T(8,128)S(1)} %get-tuple-element.30.s), channel_id=1, source_target_pairs={{0,32},{32,0},{1,33},{33,1},{2,34},{34,2},{3,35},{35,3},{4,36},{36... | collective-permute-start | bytes 786440 | tf_op jit(solution)/shard_map/ppermute | solution.py:493
  2.9 4.1 %collective-permute-start.6 = (f32[16,8,128]{2,1,0:T(8,128)S(1)}, f32[16,8,128]{2,1,0:T(8,128)S(1)}, u32[]{:S(2)}, u32[]{:S(2)}) collective-permute-start(f32[16,8,128]{2,1,0:T(8,128)S(1)} %get-tuple-element.40), channel_id=1, source_target_pairs={{0,96},{32,64},{64,32},{96,0},{1,97},{33,65},{65,33},{97,1},{2,98}... | collective-permute-start | bytes 196616 | tf_op jit(solution)/shard_map/ppermute | solution.py:492
  7.6 8.8 %collective-permute-start.8 = (f32[16,8,128]{2,1,0:T(8,128)S(1)}, f32[16,8,128]{2,1,0:T(8,128)S(1)}, u32[]{:S(2)}, u32[]{:S(2)}) collective-permute-start(f32[16,8,128]{2,1,0:T(8,128)S(1)} %shard_map.68), channel_id=1, source_target_pairs={{0,97},{97,0},{1,98},{98,1},{2,99},{99,2},{3,100},{100,3},{4,101},... | collective-permute-start | bytes 196616 | tf_op jit(solution)/shard_map/ppermute | solution.py:503
  13.6 4.9 %collective-permute-start.4 = (f32[18,8,128]{2,1,0:T(8,128)S(1)}, f32[18,8,128]{2,1,0:T(8,128)S(1)}, u32[]{:S(2)}, u32[]{:S(2)}) collective-permute-start(f32[18,8,128]{2,1,0:T(8,128)S(1)} %get-tuple-element.35), channel_id=1, source_target_pairs={{0,96},{32,64},{64,32},{96,0},{1,97},{33,65},{65,33},{97,1},{2,98}... | collective-permute-start | bytes 221192 | tf_op jit(solution)/shard_map/ppermute | solution.py:499
  16.0 5.7 %collective-permute-start.7 = (f32[16,8,128]{2,1,0:T(8,128)S(1)}, f32[16,8,128]{2,1,0:T(8,128)S(1)}, u32[]{:S(2)}, u32[]{:S(2)}) collective-permute-start(f32[16,8,128]{2,1,0:T(8,128)S(1)} %collective-permute-done.6.zo.z), channel_id=1, source_target_pairs={{0,32},{32,0},{1,33},{33,1},{2,34},{34,2},{3,35},{35,3},{4,36},{36... | collective-permute-start | bytes 196616 | tf_op jit(solution)/shard_map/ppermute | solution.py:501
  16.4 6.2 %collective-permute-start.9 = (f32[16,8,128]{2,1,0:T(8,128)S(1)}, f32[16,8,128]{2,1,0:T(8,128)S(1)}, u32[]{:S(2)}, u32[]{:S(2)}) collective-permute-start(f32[16,8,128]{2,1,0:T(8,128)S(1)} %collective-permute-done.8.b), channel_id=1, source_target_pairs={{0,32},{32,0},{1,33},{33,1},{2,34},{34,2},{3,35},{35,3},{4,36},{36... | collective-permute-start | bytes 196616 | tf_op jit(solution)/shard_map/ppermute | solution.py:504
  20.1 5.2 %collective-permute-start.5 = (f32[12,8,128]{2,1,0:T(8,128)S(1)}, f32[12,8,128]{2,1,0:T(8,128)S(1)}, u32[]{:S(2)}, u32[]{:S(2)}) collective-permute-start(f32[12,8,128]{2,1,0:T(8,128)S(1)} %get-tuple-element.39), channel_id=1, source_target_pairs={{0,96},{32,64},{64,32},{96,0},{1,97},{33,65},{65,33},{97,1},{2,98}... | collective-permute-start | bytes 147464 | tf_op jit(solution)/shard_map/ppermute | solution.py:511
  24.9 3.2 %collective-permute-start.10 = (f32[2,8,128]{2,1,0:T(8,128)S(1)}, f32[2,8,128]{2,1,0:T(8,128)S(1)}, u32[]{:S(2)}, u32[]{:S(2)}) collective-permute-start(f32[2,8,128]{2,1,0:T(8,128)S(1)} %get-tuple-element.46), channel_id=1, source_target_pairs={{0,96},{32,64},{64,32},{96,0},{1,97},{33,65},{65,33},{97,1},{2,98}... | collective-permute-start | bytes 24584 | tf_op jit(solution)/shard_map/ppermute | solution.py:519
